TPU v7x, 32 devices: a whole 2x2x4 slice. The times are simulated.
32 devices in a mesh: swath: 8 (over y, x, core), chan: 4 (over z).
Axes of the slice: x: 2, y: 2, z: 4, core: 2. Of those that a mesh axis runs over, the one named last changes fastest.
Arguments:
- innovations: float32 [524288], P(('swath', 'chan')), may hold values from -6 to 6
- obs_precision: float32 [524288], P(('swath', 'chan')), may hold values from 0.25 to 4
- jacobian: bfloat16 [524288, 128], P(('swath', 'chan')), may hold values from -0.5 to 0.5
- predictors: float32 [8, 524288], P(None, ('swath', 'chan')), may hold values from -5 to 5
- obs_column: int32 [524288], P(('swath', 'chan')), may hold values from 0 to 2047, as said below
- obs_channel: int32 [524288], P(('swath', 'chan')), may hold values from 0 to 5119
- obs_count: int32 [8, 4], P('swath', 'chan'), may hold values from 5461 to 16384, as said below
- smoothing: float32 [128], replicated, may hold values from 0.02 to 0.12
- bias_precision: float32 [8, 5120], P(None, 'chan'), may hold values from 1 to 100
Outputs:
- control_state: float32 [256, 256, 128], P('swath', 'chan')
- bias_increment: float32 [8, 5120], P(None, 'chan')
- residual_norms: float32 [3], replicated
Inputs may be any that keep to these rules, and one draw needn't show every extreme that they name: `obs_column`: Row-major index latitude row * 64 + longitude column within the tile of the device that holds the slot; all slots of an aligned block of 128 slots lie in one latitude row. `obs_channel`: channel c belongs to block c // 256, whose coefficients are owned by chan index c // 1280. `obs_count`: slots below the count hold live observations, the rest are ignored; some device is full in every draw.
All inputs are finite; a program needn't handle non-finite values.
Results may differ from a plain program's by a relative error of at most 0.0003.
Values sent between devices are 32-bit elements; how exact they have to be, the bound alone decides.
No kernel may reach another device: no remote copies, remote signals or barrier semaphores. Data moves between devices by JAX's collectives and lax.ppermute only.
A program may use at most 128 MiB of HBM per device.

v0:
```python
import functools
import jax
import jax.numpy as jnp
from jax import lax
from jax.experimental import pallas as pl
from jax.experimental.pallas import tpu as pltpu
from jax.sharding import PartitionSpec as P


LEV = 128
NPRED = 8
CH_BLOCK = 256
OBS_BLOCK = 128
LAT_DEV = 32
LON_DEV = 64
GROUP = 8
PAD = 8
UNROLL = 2
LANES = 128
SPLIT = CH_BLOCK // LANES
SHRINK = 2.0 ** -16
F32 = jnp.float32
BF16 = jnp.bfloat16
VMEM = pl.BlockSpec(memory_space=pltpu.VMEM)
SMEM = pl.BlockSpec(memory_space=pltpu.SMEM)
HBM = pl.BlockSpec(memory_space=pltpu.HBM)
NT = (((1,), (1,)), ((), ()))


def two_parts(value):
    high = value.astype(BF16)
    low = (value - high.astype(F32)).astype(BF16)
    return high, low


def dot(one, two, dims=(((1,), (0,)), ((), ()))):
    return lax.dot_general(one, two, dims, preferred_element_type=F32)


def channel_hot(channel):
    rows = lax.broadcasted_iota(jnp.int32, (CH_BLOCK, OBS_BLOCK), 0).astype(F32).astype(BF16)
    inner = jnp.bitwise_and(channel, CH_BLOCK - 1).astype(F32).astype(BF16)
    one, zero = jnp.ones_like(rows), jnp.zeros_like(rows)
    return jnp.concatenate(
        [jnp.where(rows == inner[line : line + 1], one, zero) for line in range(GROUP)], axis=1
    )


def flat_lines(value):
    return jnp.concatenate([value[line : line + 1] for line in range(GROUP)], axis=1)


def spread(terms, block_row, blocks):
    high, low = two_parts(terms)
    pieces = jnp.concatenate([high, low], axis=0)
    wide = jnp.broadcast_to(block_row, pieces.shape)
    zero = jnp.zeros_like(pieces)
    return jnp.concatenate(
        [jnp.where(wide == float(b), pieces, zero) for b in range(blocks)], axis=0
    )


def give_halves(full, mine_ref, other_ref):
    half = mine_ref.shape[0]
    odd = lax.axis_index("swath") % 2
    mine_ref[...] = full[pl.ds(odd * half, half)]
    other_ref[...] = full[pl.ds((1 - odd) * half, half)]


def put_table(out_ref, acc_ref, blocks, added):
    for b in range(blocks):
        low = 2 * NPRED * b
        total = acc_ref[low : low + NPRED] + acc_ref[low + NPRED : low + 2 * NPRED]
        for h in range(SPLIT):
            unit = SPLIT * b + h
            out_ref[unit] = total[:, h * LANES : (h + 1) * LANES] + added(unit)


def fetch(pairs, sems):
    copies = [pltpu.make_async_copy(a, b, sems.at[i]) for i, (a, b) in enumerate(pairs)]
    for copy in copies:
        copy.start()
    return copies


def chunk_copy(hbm_ref, ref, sems, i, size, axis):
    at = pl.ds(pl.multiple_of(i * size, size), size)
    where = at if axis == 0 else (slice(None), at)
    return pltpu.make_async_copy(hbm_ref.at[where], ref.at[where], sems.at[i])


def first_bias_kernel(
    count_ref, innov_hbm, prec_hbm, own_hbm, chan_hbm, col_hbm, pred_hbm,
    source_ref, weight_ref, mine_ref, other_ref, prior_ref, chan_ref, col_ref, pred_ref,
    both_ref, acc_ref, innov_ref, prec_ref, own_ref, sems, pred_sems,
):
    lines = innov_ref.shape[0]
    blocks = acc_ref.shape[0] // (4 * NPRED)
    wide_size = GROUP * OBS_BLOCK
    copies = fetch(
        [(chan_hbm, chan_ref), (innov_hbm, innov_ref), (prec_hbm, prec_ref), (own_hbm, own_ref)], sems
    )

    def start(i, _):
        chunk_copy(pred_hbm, pred_ref, pred_sems, i, wide_size, 1).start()
        return 0

    lax.fori_loop(0, lines // GROUP, start, 0)
    late = [pltpu.make_async_copy(col_hbm, col_ref, sems.at[4])]
    for copy in late:
        copy.start()
    acc_ref[...] = jnp.zeros_like(acc_ref)
    prior_ref[...] = jnp.zeros_like(prior_ref)
    for copy in copies:
        copy.wait()

    @pl.when(lax.axis_index("swath") == 0)
    def _():
        units = own_ref.shape[1] // LANES
        for j in range(units):
            prior_ref[lax.axis_index("chan") * units + j] = own_ref[:, j * LANES : (j + 1) * LANES]

    def step(i, _):
        chunk_copy(pred_hbm, pred_ref, pred_sems, i, wide_size, 1).wait()
        at = pl.ds(pl.multiple_of(i * GROUP, GROUP), GROUP)
        wide = pl.ds(pl.multiple_of(i * wide_size, wide_size), wide_size)
        slot = (
            (i * GROUP + lax.broadcasted_iota(jnp.int32, (GROUP, OBS_BLOCK), 0)) * OBS_BLOCK
            + lax.broadcasted_iota(jnp.int32, (GROUP, OBS_BLOCK), 1)
        )
        weight = jnp.where(slot < count_ref[0, 0], prec_ref[at], 0.0)
        source = weight * innov_ref[at]
        weight_ref[at] = weight
        source_ref[at] = source
        channel = chan_ref[at]
        hot = channel_hot(channel)
        block_row = flat_lines(lax.shift_right_logical(channel, 8).astype(F32)).astype(BF16)
        pred = pred_ref[:, wide]
        terms = spread(pred * flat_lines(source), block_row, blocks)
        squares = spread(pred * pred * flat_lines(weight), block_row, blocks)
        acc_ref[...] += dot(jnp.concatenate([terms, squares], axis=0), hot, NT)
        return 0

    lax.fori_loop(0, lines // GROUP, step, 0)
    put_table(both_ref.at[0], acc_ref, blocks, lambda unit: 0.0)
    put_table(both_ref.at[1], acc_ref.at[pl.ds(2 * NPRED * blocks, 2 * NPRED * blocks)], blocks, lambda unit: prior_ref[unit])
    for k in range(2):
        give_halves(both_ref.at[k], mine_ref.at[k], other_ref.at[k])
    for copy in late:
        copy.wait()


def bias_kernel(
    image_ref, weight_ref, prior_ref, mine_ref, other_ref, chan_ref, pred_ref,
    value_ref, keep_ref, send_ref, table_ref, acc_ref, look_ref, full_ref,
):
    lines = image_ref.shape[0]
    blocks = acc_ref.shape[0] // (2 * NPRED)
    wide_size = GROUP * OBS_BLOCK
    acc_ref[...] = jnp.zeros_like(acc_ref)
    half = mine_ref.shape[0]
    odd = lax.axis_index("swath") % 2
    full_ref[pl.ds(odd * half, half)] = mine_ref[...]
    full_ref[pl.ds((1 - odd) * half, half)] = other_ref[...]
    for b in range(blocks):
        coef = jnp.concatenate([full_ref[SPLIT * b + h] for h in range(SPLIT)], axis=1)
        high, low = two_parts(coef)
        look_ref[2 * NPRED * b : 2 * NPRED * (b + 1)] = jnp.concatenate([high, low], axis=0)

    def at(i):
        return pl.ds(pl.multiple_of(i * GROUP, GROUP), GROUP)

    def wide(i):
        return pl.ds(pl.multiple_of(i * wide_size, wide_size), wide_size)

    def block_of(channel):
        return flat_lines(lax.shift_right_logical(channel, 8).astype(F32))

    def look(i):
        channel = chan_ref[at(i)]
        pred = pred_ref[:, wide(i)]
        found = dot(look_ref[...], channel_hot(channel))
        block_wide = jnp.broadcast_to(block_of(channel), pred.shape)
        picked = jnp.zeros_like(pred)
        for b in range(blocks):
            low = 2 * NPRED * b
            both = found[low : low + NPRED] + found[low + NPRED : low + 2 * NPRED]
            picked = jnp.where(block_wide == float(b), both, picked)
        looked = jnp.sum(picked * pred, axis=0, keepdims=True)
        looked = jnp.concatenate(
            [looked[:, j * OBS_BLOCK : (j + 1) * OBS_BLOCK] for j in range(GROUP)], axis=0
        )
        value = weight_ref[at(i)] * (image_ref[at(i)] + looked)
        value_ref[at(i)] = value
        return value

    def tell(i, value):
        channel = chan_ref[at(i)]
        terms = pred_ref[:, wide(i)] * flat_lines(value)
        spreads = spread(terms, block_of(channel).astype(BF16), blocks)
        acc_ref[...] += dot(spreads, channel_hot(channel), NT)

    def step(i, value):
        following = look(i)
        tell(i - 1, value)
        return following

    last = lines // GROUP - 1
    tell(last, lax.fori_loop(1, last + 1, step, look(0)))
    put_table(table_ref, acc_ref, blocks, lambda unit: prior_ref[unit] * full_ref[unit])
    give_halves(table_ref, keep_ref, send_ref)


def add_kernel(one_ref, two_ref, out_ref):
    out_ref[...] = one_ref[...] + two_ref[...]


def split_add_kernel(mask, one_ref, two_ref, keep_ref, send_ref):
    half = keep_ref.shape[0]
    bit = (lax.axis_index("swath") // mask) % 2
    keep, send = pl.ds(bit * half, half), pl.ds((1 - bit) * half, half)
    keep_ref[...] = one_ref[keep] + two_ref[keep]
    send_ref[...] = one_ref[send] + two_ref[send]


def first_ratio_kernel(one_ref, two_ref, r_ref, diag_ref, z_ref):
    r = one_ref[0] + two_ref[0]
    diag = one_ref[1] + two_ref[1]
    r_ref[...] = r
    diag_ref[...] = diag
    z_ref[...] = r / diag


def ratio_kernel(one_ref, two_ref, diag_ref, w_ref, u_ref):
    w = (one_ref[...] + two_ref[...]) * SHRINK
    w_ref[...] = w
    u_ref[...] = w / diag_ref[...]


def start_jac(jac_hbm, jac_ref, sems):
    def start(i, _):
        chunk_copy(jac_hbm, jac_ref, sems, i, GROUP * OBS_BLOCK, 0).start()
        return 0

    lax.fori_loop(0, jac_ref.shape[0] // (GROUP * OBS_BLOCK), start, 0)


def adjoint_kernel(scale, has_base, width, first, last, row_ref, value_ref, col_ref, jac_ref, *rest):
    out_ref = rest[-3] if width else rest[-1]
    if not has_base:
        out_ref[...] = jnp.zeros_like(out_ref)
    cells = lax.broadcasted_iota(jnp.int32, (LON_DEV, OBS_BLOCK), 0)

    def step(i, _):
        at = pl.ds(pl.multiple_of(i * GROUP, GROUP), GROUP)
        value = value_ref[at]
        high = value.astype(BF16).astype(F32)
        low = value - high
        col = jnp.bitwise_and(col_ref[at], LON_DEV - 1)
        for j in range(GROUP):
            hit = cells == col[j : j + 1]
            left = jnp.concatenate(
                [jnp.where(hit, high[j : j + 1], 0.0), jnp.where(hit, low[j : j + 1], 0.0)], axis=0
            ).astype(BF16)
            line = i * GROUP + j
            jac = jac_ref[pl.ds(pl.multiple_of(line * OBS_BLOCK, OBS_BLOCK), OBS_BLOCK), :]
            got = dot(left, jac)
            row = row_ref[line]
            out_ref[row] += got[:LON_DEV] + got[LON_DEV:]
        return 0

    lax.fori_loop(first, last, step, 0, unroll=UNROLL)
    if scale != 1.0:
        out_ref[...] = out_ref[...] * scale
    if width:
        near_ref, far_ref = rest[-2:]
        odd = lax.axis_index("swath") % 2 == 1
        count = out_ref.shape[0]

        @pl.when(odd)
        def _():
            near_ref[...] = out_ref[:width]
            far_ref[...] = out_ref[count - width :]

        @pl.when(jnp.logical_not(odd))
        def _():
            near_ref[...] = out_ref[count - width :]
            far_ref[...] = out_ref[:width]

        band = lax.axis_index("swath")

        @pl.when((band == 0) | (band == lax.axis_size("swath") - 1))
        def _():
            far_ref[...] = jnp.zeros_like(far_ref)


def edge_kernel(g_ref, near_ref, far_ref, beside_ref, across_ref):
    rows, width = g_ref.shape[0], near_ref.shape[0]
    left, right = slice(0, width), slice(LON_DEV - width, LON_DEV)
    odd_band = lax.axis_index("swath") % 2 == 1
    odd_sector = lax.axis_index("chan") % 2 == 1

    def put(ref, cut):
        ref[width : width + rows] = g_ref[:, cut]

        @pl.when(odd_band)
        def _():
            ref[:width] = near_ref[:, cut]
            ref[width + rows :] = far_ref[:, cut]

        @pl.when(jnp.logical_not(odd_band))
        def _():
            ref[:width] = far_ref[:, cut]
            ref[width + rows :] = near_ref[:, cut]

    @pl.when(odd_sector)
    def _():
        put(beside_ref, left)
        put(across_ref, right)

    @pl.when(jnp.logical_not(odd_sector))
    def _():
        put(beside_ref, right)
        put(across_ref, left)


def fill_padded(pad_ref, g_ref, near_ref, far_ref, beside_ref, across_ref, width):
    rows = g_ref.shape[0]
    inside = slice(PAD, PAD + LON_DEV)
    above, below = slice(0, width), slice(width + rows, 2 * width + rows)
    west, east = slice(PAD - width, PAD), slice(PAD + LON_DEV, PAD + LON_DEV + width)
    pad_ref[width : width + rows, inside] = g_ref[...]
    odd_band = lax.axis_index("swath") % 2 == 1
    odd_sector = lax.axis_index("chan") % 2 == 1

    @pl.when(odd_band)
    def _():
        pad_ref[above, inside] = near_ref[...]
        pad_ref[below, inside] = far_ref[...]

    @pl.when(jnp.logical_not(odd_band))
    def _():
        pad_ref[above, inside] = far_ref[...]
        pad_ref[below, inside] = near_ref[...]

    @pl.when(odd_sector)
    def _():
        pad_ref[:, west] = beside_ref[...]
        pad_ref[:, east] = across_ref[...]

    @pl.when(jnp.logical_not(odd_sector))
    def _():
        pad_ref[:, west] = across_ref[...]
        pad_ref[:, east] = beside_ref[...]


def smoothed_row(pad_ref, row, smooth):
    here = pad_ref[row]
    size = here.shape[0]
    beside = (
        pad_ref[row - 1]
        + pad_ref[row + 1]
        + pltpu.roll(here, 1, 0)
        + pltpu.roll(here, size - 1, 0)
    )
    return here + smooth * (beside - 4.0 * here)


def forward_kernel(
    row_ref, smooth_ref, g_ref, near_ref, far_ref, beside_ref, across_ref, col_ref, jac_hbm,
    image_ref, z_ref, pad_ref, zpad_ref, part_ref, jac_ref, sems,
):
    rows = g_ref.shape[0]
    lines = col_ref.shape[0]
    smooth = smooth_ref[...]
    start_jac(jac_hbm, jac_ref, sems)
    fill_padded(pad_ref, g_ref, near_ref, far_ref, beside_ref, across_ref, 2)

    def first(r, _):
        zpad_ref[r] = smoothed_row(pad_ref, r + 1, smooth)
        return 0

    lax.fori_loop(0, rows + 2, first, 0, unroll=2)

    @pl.when(lax.axis_index("swath") == 0)
    def _():
        zpad_ref[0] = jnp.zeros_like(zpad_ref[0])

    @pl.when(lax.axis_index("swath") == lax.axis_size("swath") - 1)
    def _():
        zpad_ref[rows + 1] = jnp.zeros_like(zpad_ref[0])

    z_ref[...] = zpad_ref[1 : rows + 1, PAD : PAD + LON_DEV]

    def second(r, _):
        high, low = two_parts(smoothed_row(zpad_ref, r + 1, smooth)[PAD : PAD + LON_DEV])
        part_ref[r] = jnp.concatenate([high, low], axis=0)
        return 0

    lax.fori_loop(0, rows, second, 0, unroll=2)
    cells = lax.broadcasted_iota(jnp.int32, (LON_DEV, OBS_BLOCK), 0)

    def step(i, _):
        chunk_copy(jac_hbm, jac_ref, sems, i, GROUP * OBS_BLOCK, 0).wait()
        at = pl.ds(pl.multiple_of(i * GROUP, GROUP), GROUP)
        col = jnp.bitwise_and(col_ref[at], LON_DEV - 1)
        found = []
        for j in range(GROUP):
            line = i * GROUP + j
            jac = jac_ref[pl.ds(pl.multiple_of(line * OBS_BLOCK, OBS_BLOCK), OBS_BLOCK), :]
            got = dot(part_ref[row_ref[line]], jac, NT)
            both = got[:LON_DEV] + got[LON_DEV:]
            found.append(
                jnp.sum(jnp.where(cells == col[j : j + 1], both, 0.0), axis=0, keepdims=True)
            )
        image_ref[at] = jnp.concatenate(found, axis=0)
        return 0

    lax.fori_loop(0, lines // GROUP, step, 0, unroll=UNROLL)


def gram_kernel(
    share, cuts, smooth_ref, g_ref, near_ref, far_ref, beside_ref, across_ref, z_ref, w_ref,
    rb_ref, zb_ref, wb_ref, ub_ref, one_ref, two_ref, sum_ref, pad_ref,
):
    rows = g_ref.shape[0]
    smooth = smooth_ref[...]
    fill_padded(pad_ref, g_ref, near_ref, far_ref, beside_ref, across_ref, 1)

    def step(r, sums):
        z = z_ref[r]
        w = w_ref[r]
        v = smoothed_row(pad_ref, r + 1, smooth)[PAD : PAD + LON_DEV]
        made = []
        for total, (one, two) in zip(sums, ((z, z), (z, w), (w, w), (z, v), (w, v), (v, v))):
            made.append(total + jnp.sum((one * two).reshape(LON_DEV // 8, 8, LEV), axis=0))
        return tuple(made)

    zero = jnp.zeros((8, LEV), F32)
    zz, zw, ww, zv, wv, vv = lax.fori_loop(0, rows, step, (zero,) * 6)
    offset = 0
    for mask, size in cuts:
        offset = offset + (lax.axis_index("swath") // mask) % 2 * size
    own = pl.ds(offset, one_ref.shape[0])
    rb, zb, wb, ub = (ref[own] for ref in (rb_ref, zb_ref, wb_ref, ub_ref))
    vb = one_ref[...] + two_ref[...]
    lane = lax.broadcasted_iota(jnp.int32, (8, LANES), 1)
    sums = jnp.zeros((8, LANES), F32)
    pairs = (
        (zz, rb, rb), (zz, rb, zb), (zw, zb, wb), (zw, rb, wb), (ww, wb, ub),
        (ww, wb, wb), (wv, ub, vb), (zv, rb, vb), (wv, wb, vb), (vv, vb, vb),
    )
    for k, (state, one, two) in enumerate(pairs):
        both = state + jnp.sum(one * two, axis=0) * share
        both = jnp.sum(jnp.sum(both, axis=0, keepdims=True), axis=1, keepdims=True)
        sums = jnp.where(lane == k, both, sums)
    sum_ref[...] = jnp.broadcast_to(sums[None], sum_ref.shape)


def final_kernel(
    sum_ref, z_ref, w_ref, zm_ref, zo_ref, um_ref, uo_ref, x_ref, xb_ref, norm_ref
):
    sums = jnp.sum(sum_ref[...], axis=0)[:1]
    lane = lax.broadcasted_iota(jnp.int32, (1, LANES), 1)
    rr, rz, zw, rw, wu, ww, uv, rv, wv, vv = (
        jnp.sum(jnp.where(lane == k, sums, 0.0), axis=1, keepdims=True) for k in range(10)
    )
    grow = 1.0 / SHRINK
    first = rz / (zw * grow)
    big = first * grow
    rz_one = rz - 2.0 * big * zw + big * big * wu
    rr_one = rr - 2.0 * big * rw + big * big * ww
    ratio = rz_one / rz
    lift = 1.0 + ratio
    curve = lift * lift * (zw * grow) - 2.0 * lift * first * wu * (grow * grow) + big * big * uv
    second = rz_one / curve
    main = first + second * lift
    side = first * second * grow
    main_big = main * grow
    rr_two = (
        rr + main_big * main_big * ww + side * side * vv
        - 2.0 * main_big * rw + 2.0 * side * rv - 2.0 * main_big * side * wv
    )
    x_ref[...] = main[:, None] * z_ref[...] - side[:, None] * w_ref[...]
    half = zm_ref.shape[0]
    units = xb_ref.shape[1] // LANES
    for j in range(units):
        unit = lax.axis_index("chan") * units + j
        upper = (unit >= half).astype(jnp.int32)
        at = unit - upper * half
        here = upper == lax.axis_index("swath") % 2
        z_unit = jnp.where(here, zm_ref[at], zo_ref[at])
        u_unit = jnp.where(here, um_ref[at], uo_ref[at])
        xb_ref[:, j * LANES : (j + 1) * LANES] = main * z_unit - side * u_unit
    squares = jnp.where(lane == 0, rr, jnp.where(lane == 1, rr_one, rr_two))
    norm_ref[...] = jnp.sqrt(jnp.maximum(squares, 0.0))[:, : norm_ref.shape[1]]


def call(kernel, outs, scratch=(), flops=0, smem=(), hbm=(), limit=12 << 20, alias=None):
    shapes = [jax.ShapeDtypeStruct(s, d) for s, d in outs]

    def place_call(*args):
        count = len(args)
        far = [i % count for i in hbm]
        args = [
            pltpu.with_memory_space_constraint(a, pltpu.HBM) if i in far else a
            for i, a in enumerate(args)
        ]
        specs = [SMEM if i in smem else HBM if i in far else VMEM for i in range(count)]
        return pl.pallas_call(
            kernel,
            out_shape=shapes,
            in_specs=specs,
            out_specs=[VMEM] * len(shapes),
            scratch_shapes=list(scratch),
            input_output_aliases=alias or {},
            cost_estimate=pl.CostEstimate(flops=flops, transcendentals=0, bytes_accessed=1 << 20),
            compiler_params=pltpu.CompilerParams(vmem_limit_bytes=limit),
        )(*args)

    return place_call


def trade(value, axis, mask):
    size = lax.axis_size(axis)
    return lax.ppermute(value, axis, [(i, i ^ mask) for i in range(size)])


def powers(start, size):
    while start < size:
        yield start
        start *= 2


def add(one, two):
    return call(add_kernel, [(one.shape, F32)], limit=1 << 20)(one, two)[0]


def chips_sum(mine):
    parts = []
    for axis, start in (("swath", 2), ("chan", 1)):
        for m in powers(start, lax.axis_size(axis)):
            parts.append((axis, m))
    for axis, m in parts[:-1]:
        mine = add(mine, trade(mine, axis, m))
    axis, m = parts[-1]
    return mine, trade(mine, axis, m)


def chips_scatter(mine, got):
    parts = [("swath", m) for m in powers(2, lax.axis_size("swath"))]
    parts += [("chan", m) for m in powers(1, lax.axis_size("chan"))]
    cuts = []
    for axis, m in parts:
        units = mine.shape[0]
        if axis == "swath" and units % 2 == 0:
            half = (units // 2,) + mine.shape[1:]
            kernel = functools.partial(split_add_kernel, m)
            mine, sent = call(kernel, [(half, F32)] * 2, limit=1 << 20)(mine, got)
            cuts.append((m, units // 2))
        else:
            sent = mine = add(mine, got)
        got = trade(sent, axis, m)
    return (mine, got), cuts


def halos(g, near, far):
    bands, sectors = lax.axis_size("swath"), lax.axis_size("chan")
    rows, width = g.shape[0], near.shape[0]
    near = trade(near, "swath", 1)
    pairs = [(i, (i + 1) % bands) for i in range(1, bands, 2)]
    far = lax.ppermute(far, "swath", pairs + [(j, i) for i, j in pairs])
    edge = ((rows + 2 * width, width, LEV), F32)
    beside, across = call(edge_kernel, [edge, edge], limit=4 << 20)(g, near, far)
    beside = trade(beside, "chan", 1)
    pairs = [(i, (i + 1) % sectors) for i in range(1, sectors, 2)]
    across = lax.ppermute(across, "chan", pairs + [(j, i) for i, j in pairs])
    return g, near, far, beside, across


def body(
    innovations, obs_precision, jacobian, predictors, obs_column, obs_channel, obs_count,
    smoothing, bias_precision,
):
    slots = obs_precision.shape[0]
    lines = slots // OBS_BLOCK
    chunks = lines // GROUP
    owned = bias_precision.shape[1]
    bands, sectors = lax.axis_size("swath"), lax.axis_size("chan")
    channels = owned * sectors
    blocks = channels // CH_BLOCK
    units = channels // LANES
    smooth = smoothing.reshape(1, LEV)
    by_line = (lines, OBS_BLOCK)
    col = obs_column.reshape(by_line)
    channel = obs_channel.reshape(by_line)
    rows = col[:, 0] // LON_DEV
    tile = (LAT_DEV, LON_DEV, LEV)
    table = (units, NPRED, LANES)
    wide = LON_DEV + 2 * PAD
    acc = pltpu.VMEM((2 * NPRED * blocks, CH_BLOCK), F32)
    hot_flops = 2 * 2 * NPRED * blocks * CH_BLOCK * slots
    tile_flops = 4 * LON_DEV * LEV * slots
    line_out = (by_line, F32)
    line_f32 = pltpu.VMEM(by_line, F32)
    sems = lambda count: pltpu.SemaphoreType.DMA((count,))

    jac_space = [pltpu.VMEM((slots, LEV), BF16), sems(chunks)]

    half = (units // 2, NPRED, LANES)
    pair = (2,) + half
    first_bias = call(
        first_bias_kernel,
        [
            line_out, line_out, (pair, F32), (pair, F32), (table, F32), (by_line, jnp.int32),
            (by_line, jnp.int32), (predictors.shape, F32),
        ],
        [
            pltpu.VMEM((2,) + table, F32), pltpu.VMEM((4 * NPRED * blocks, CH_BLOCK), F32),
            line_f32, line_f32,
            pltpu.VMEM((NPRED, owned), F32), sems(5), sems(chunks),
        ],
        2 * hot_flops, (0,), range(1, 7),
    )
    bias = call(
        bias_kernel, [line_out, (half, F32), (half, F32)],
        [
            pltpu.VMEM(table, F32), acc, pltpu.VMEM((2 * NPRED * blocks, CH_BLOCK), BF16),
            pltpu.VMEM(table, F32),
        ],
        2 * hot_flops,
    )

    def adjoint(value, base, scale, width):
        kernel = functools.partial(adjoint_kernel, scale, base is not None, width, 0, chunks)
        args = (rows, value, col, jacobian) + (() if base is None else (base,))
        return call(
            kernel, [(tile, F32)] + [((width, LON_DEV, LEV), F32)] * 2, (), tile_flops, (0,),
            alias=None if base is None else {4: 0},
        )(*args)

    forward = lambda: call(
        forward_kernel, [line_out, (tile, F32)],
        [
            pltpu.VMEM((LAT_DEV + 4, wide, LEV), F32),
            pltpu.VMEM((LAT_DEV + 2, wide, LEV), F32),
            pltpu.VMEM((LAT_DEV, 2 * LON_DEV, LEV), BF16),
            *jac_space,
        ],
        tile_flops, (0,), (-1,),
    )

    source, weight, mine, other, prior, channel, col, pred = first_bias(
        obs_count, innovations.reshape(by_line), obs_precision.reshape(by_line),
        bias_precision, channel, col, predictors,
    )
    both = add(mine, trade(other, "swath", 1))
    g0 = adjoint(source, None, 1.0, 2)
    rb, diag, zb = call(first_ratio_kernel, [(half, F32)] * 3, limit=2 << 20)(*chips_sum(both))
    zo = trade(zb, "swath", 1)
    image, z = forward()(rows, smooth, *halos(*g0), col, jacobian)
    value, mine, other = bias(image, weight, prior, zb, zo, channel, pred)
    wb = add(mine, trade(other, "swath", 1))
    g1 = adjoint(value, g0[0], SHRINK, 2)
    wb, ub = call(ratio_kernel, [(half, F32)] * 2, limit=2 << 20)(*chips_sum(wb), diag)
    uo = trade(ub, "swath", 1)
    image, w = forward()(rows, smooth, *halos(*g1), col, jacobian)
    value, mine, other = bias(image, weight, prior, ub, uo, channel, pred)
    got = trade(other, "swath", 1)
    g2 = adjoint(value, g1[0], 1.0, 1)
    parts, cuts = chips_scatter(mine, got)
    copies = bands * sectors * parts[0].shape[0] // units
    gram = call(
        functools.partial(gram_kernel, 1.0 / copies, cuts), [((bands * sectors, 8, LANES), F32)],
        [pltpu.VMEM((LAT_DEV + 2, wide, LEV), F32)], 1 << 22,
    )
    sums = gram(smooth, *halos(*g2), z, w, rb, zb, wb, ub, *parts)[0]
    sums = lax.all_to_all(sums, ("swath", "chan"), 0, 0)
    x, xb, norms = call(
        final_kernel, [(tile, F32), ((NPRED, owned), F32), ((1, 3), F32)],
    )(sums, z, w, zb, zo, ub, uo)
    return x, xb, norms.reshape(3)


def solution(mesh):
    placed = (
        P(("swath", "chan")),
        P(("swath", "chan")),
        P(("swath", "chan"), None),
        P(None, ("swath", "chan")),
        P(("swath", "chan")),
        P(("swath", "chan")),
        P("swath", "chan"),
        P(),
        P(None, "chan"),
    )
    return jax.shard_map(
        body,
        mesh=mesh,
        in_specs=placed,
        out_specs=(P("swath", "chan", None), P(None, "chan"), P()),
        check_vma=False,
    )
```

profile of v0, /device:TPU:0, one launch (start us, length us, event | category | flops | bytes accessed | tf_op | source)
XLA Modules:
  0.0 148.2 jit_solution(10013216809326249400)
XLA Ops:
  1.3 10.1 %shard_map.112 = (f32[128,128]{1,0:T(8,128)S(1)}, f32[128,128]{1,0:T(8,128)S(1)}, f32[2,20,8,128]{3,2,1,0:T(8,128)S(1)}, f32[2,20,8,128]{3,2,1,0:T(8,128)S(1)}, ...) custom-call(s32[1,1]{1,0:T(1,128)S(6)} %copy.16.count_ref, ...), custom_call_target="tpu_custom_call" | custom-call | flops 5368709120 | bytes 1048576 | tf_op jit(solution)/shard_map/pallas_call | solution.py:510
  11.5 0.5 collective-permute-start.4
  12.0 1.0 collective-permute-done.4.two_ref
  13.1 2.8 %collective-permute-start.5 = (f32[2,20,8,128]{3,2,1,0:T(8,128)S(1)}, f32[2,20,8,128]{3,2,1,0:T(8,128)S(1)}, u32[]{:S(2)}, u32[]{:S(2)}) collective-permute-start(f32[2,20,8,128]{3,2,1,0:T(8,128)S(1)} %shard_map.116.one_ref), channel_id=1, source_target_pairs={{0,8},{4,12},{8,0},{12,4},{16,24},{20,28},{24,16},{28,20},{1,9},{5... | collective-permute-start | bytes 491528 | tf_op jit(solution)/shard_map/ppermute | solution.py:526
  15.9 4.5 %collective-permute-done.5.two_ref = f32[2,20,8,128]{3,2,1,0:T(8,128)S(1)} collective-permute-done((f32[2,20,8,128]{3,2,1,0:T(8,128)S(1)}, f32[2,20,8,128]{3,2,1,0:T(8,128)S(1)}, u32[]{:S(2)}, u32[]{:S(2)}) %collective-permute-start.5) | collective-permute-done | bytes 163872 | tf_op jit(solution)/shard_map/ppermute | solution.py:526
  20.4 2.0 %collective-permute-start.6 = (f32[2,20,8,128]{3,2,1,0:T(8,128)S(1)}, f32[2,20,8,128]{3,2,1,0:T(8,128)S(1)}, u32[]{:S(2)}, u32[]{:S(2)}) collective-permute-start(f32[2,20,8,128]{3,2,1,0:T(8,128)S(1)} %shard_map.117.one_ref), channel_id=1, source_target_pairs={{0,16},{4,20},{8,24},{12,28},{16,0},{20,4},{24,8},{28,12},{1,17},{... | collective-permute-start | bytes 491528 | tf_op jit(solution)/shard_map/ppermute | solution.py:526
  22.4 3.8 %collective-permute-done.6.two_ref = f32[2,20,8,128]{3,2,1,0:T(8,128)S(1)} collective-permute-done((f32[2,20,8,128]{3,2,1,0:T(8,128)S(1)}, f32[2,20,8,128]{3,2,1,0:T(8,128)S(1)}, u32[]{:S(2)}, u32[]{:S(2)}) %collective-permute-start.6) | collective-permute-done | bytes 163872 | tf_op jit(solution)/shard_map/ppermute | solution.py:526
  26.2 1.7 %collective-permute-start.7 = (f32[2,20,8,128]{3,2,1,0:T(8,128)S(1)}, f32[2,20,8,128]{3,2,1,0:T(8,128)S(1)}, u32[]{:S(2)}, u32[]{:S(2)}) collective-permute-start(f32[2,20,8,128]{3,2,1,0:T(8,128)S(1)} %shard_map.118.one_ref), channel_id=1, source_target_pairs={{0,1},{1,0},{2,3},{3,2},{4,5},{5,4},{6,7},{7,6},{8,9},{9,8},{10,11... | collective-permute-start | bytes 491528 | tf_op jit(solution)/shard_map/ppermute | solution.py:526
  28.0 3.6 %collective-permute-done.7.two_ref = f32[2,20,8,128]{3,2,1,0:T(8,128)S(1)} collective-permute-done((f32[2,20,8,128]{3,2,1,0:T(8,128)S(1)}, f32[2,20,8,128]{3,2,1,0:T(8,128)S(1)}, u32[]{:S(2)}, u32[]{:S(2)}) %collective-permute-start.7) | collective-permute-done | bytes 163872 | tf_op jit(solution)/shard_map/ppermute | solution.py:526
  31.6 2.9 %collective-permute-start.8 = (f32[2,20,8,128]{3,2,1,0:T(8,128)S(1)}, f32[2,20,8,128]{3,2,1,0:T(8,128)S(1)}, u32[]{:S(2)}, u32[]{:S(2)}) collective-permute-start(f32[2,20,8,128]{3,2,1,0:T(8,128)S(1)} %shard_map.119.one_ref), channel_id=1, source_target_pairs={{0,2},{1,3},{2,0},{3,1},{4,6},{5,7},{6,4},{7,5},{8,10},{9,11},{10,... | collective-permute-start | bytes 491528 | tf_op jit(solution)/shard_map/ppermute | solution.py:526
  34.5 3.0 %shard_map.113 = (f32[32,64,128]{2,1,0:T(8,128)S(1)}, f32[2,64,128]{2,1,0:T(8,128)S(1)}, f32[2,64,128]{2,1,0:T(8,128)S(1)}) custom-call(s32[128]{0:T(128)S(1)} %and_select_fusion.row_ref, f32[128,128]{1,0:T(8,128)S(1)} %get-tuple-element.48.value_ref, s32[128,128]{1,0:T(8,128)S(1)} %get-tuple-element.49.col_ref, bf16[16384,128]{1,0:T(8,128)(2,1)S(1)} %copy-done), custom_call_target="tpu_custom_call" | custom-call | flops 536870912 | bytes 1048576 | tf_op jit(solution)/shard_map/pallas_call | solution.py:510
  37.6 2.7 %collective-permute-start.1 = (f32[2,64,128]{2,1,0:T(8,128)S(1)}, f32[2,64,128]{2,1,0:T(8,128)S(1)}, u32[]{:S(2)}, u32[]{:S(2)}) collective-permute-start(f32[2,64,128]{2,1,0:T(8,128)S(1)} %get-tuple-element.52), channel_id=1, source_target_pairs={{4,8},{12,16},{20,24},{28,0},{8,4},{16,12},{24,20},{0,28},{5,9},{1... | collective-permute-start | bytes 196616 | tf_op jit(solution)/shard_map/ppermute | solution.py:572
  40.3 2.0 %collective-permute-done.1.far_ref = f32[2,64,128]{2,1,0:T(8,128)S(1)} collective-permute-done((f32[2,64,128]{2,1,0:T(8,128)S(1)}, f32[2,64,128]{2,1,0:T(8,128)S(1)}, u32[]{:S(2)}, u32[]{:S(2)}) %collective-permute-start.1) | collective-permute-done | bytes 65568 | tf_op jit(solution)/shard_map/ppermute | solution.py:572
  42.3 1.5 %collective-permute-start.2 = (f32[36,2,128]{2,1,0:T(2,128)S(1)}, f32[36,2,128]{2,1,0:T(2,128)S(1)}, u32[]{:S(2)}, u32[]{:S(2)}) collective-permute-start(f32[36,2,128]{2,1,0:T(2,128)S(1)} %get-tuple-element.53), channel_id=1, source_target_pairs={{0,1},{1,0},{2,3},{3,2},{4,5},{5,4},{6,7},{7,6},{8,9},{9,8},{10,11... | collective-permute-start | bytes 110600 | tf_op jit(solution)/shard_map/ppermute | solution.py:526
  43.8 0.1 collective-permute-start.3
  44.1 2.2 %collective-permute-done.2.beside_ref = f32[36,2,128]{2,1,0:T(2,128)S(1)} collective-permute-done((f32[36,2,128]{2,1,0:T(2,128)S(1)}, f32[36,2,128]{2,1,0:T(2,128)S(1)}, u32[]{:S(2)}, u32[]{:S(2)}) %collective-permute-start.2) | collective-permute-done | bytes 36896 | tf_op jit(solution)/shard_map/ppermute | solution.py:526
  46.3 3.3 %collective-permute-done.3.across_ref = f32[36,2,128]{2,1,0:T(2,128)S(1)} collective-permute-done((f32[36,2,128]{2,1,0:T(2,128)S(1)}, f32[36,2,128]{2,1,0:T(2,128)S(1)}, u32[]{:S(2)}, u32[]{:S(2)}) %collective-permute-start.3) | collective-permute-done | bytes 36896 | tf_op jit(solution)/shard_map/ppermute | solution.py:577
  49.6 7.2 %shard_map.115 = (f32[128,128]{1,0:T(8,128)S(1)}, f32[32,64,128]{2,1,0:T(8,128)S(1)}) custom-call(s32[128]{0:T(128)S(1)} %and_select_fusion.row_ref, f32[1,128]{1,0:T(1,128)S(1)} %bitcast.6, f32[32,64,128]{2,1,0:T(8,128)S(1)} %get-tuple-element.50.g_ref.rest_0_, f32[2,64,128]{2,1,0:T(8,128)S(1)} %collective-permute-done.near_ref, ...), custom_call_target="tpu_custom_call" | custom-call | flops 536870912 | bytes 1048576 | tf_op jit(solution)/shard_map/pallas_call | solution.py:510
  56.8 8.6 %shard_map.121 = (f32[128,128]{1,0:T(8,128)S(1)}, f32[20,8,128]{2,1,0:T(8,128)S(1)}, f32[20,8,128]{2,1,0:T(8,128)S(1)}) custom-call(f32[128,128]{1,0:T(8,128)S(1)} %get-tuple-element.55.image_ref, f32[128,128]{1,0:T(8,128)S(1)} %get-tuple-element.56.weight_ref, f32[40,8,128]{2,1,0:T(8,128)S(1)} %get-tuple-element.57.prior_ref, ...), custom_call_target="tpu_custom_call" | custom-call | flops 5368709120 | bytes 1048576 | tf_op jit(solution)/shard_map/pallas_call | solution.py:510
  65.4 1.3 collective-permute-done.14.two_ref
  66.7 0.8 collective-permute-start.15
  67.5 3.7 %collective-permute-done.15.two_ref = f32[20,8,128]{2,1,0:T(8,128)S(1)} collective-permute-done((f32[20,8,128]{2,1,0:T(8,128)S(1)}, f32[20,8,128]{2,1,0:T(8,128)S(1)}, u32[]{:S(2)}, u32[]{:S(2)}) %collective-permute-start.15) | collective-permute-done | bytes 81952 | tf_op jit(solution)/shard_map/ppermute | solution.py:526
  71.3 1.9 %collective-permute-start.16 = (f32[20,8,128]{2,1,0:T(8,128)S(1)}, f32[20,8,128]{2,1,0:T(8,128)S(1)}, u32[]{:S(2)}, u32[]{:S(2)}) collective-permute-start(f32[20,8,128]{2,1,0:T(8,128)S(1)} %shard_map.126.one_ref), channel_id=1, source_target_pairs={{0,16},{4,20},{8,24},{12,28},{16,0},{20,4},{24,8},{28,12},{1,17},{... | collective-permute-start | bytes 245768 | tf_op jit(solution)/shard_map/ppermute | solution.py:526
  73.2 2.6 %collective-permute-done.16.two_ref = f32[20,8,128]{2,1,0:T(8,128)S(1)} collective-permute-done((f32[20,8,128]{2,1,0:T(8,128)S(1)}, f32[20,8,128]{2,1,0:T(8,128)S(1)}, u32[]{:S(2)}, u32[]{:S(2)}) %collective-permute-start.16) | collective-permute-done | bytes 81952 | tf_op jit(solution)/shard_map/ppermute | solution.py:526
  75.9 4.4 %collective-permute-done.17.two_ref = f32[20,8,128]{2,1,0:T(8,128)S(1)} collective-permute-done((f32[20,8,128]{2,1,0:T(8,128)S(1)}, f32[20,8,128]{2,1,0:T(8,128)S(1)}, u32[]{:S(2)}, u32[]{:S(2)}) %collective-permute-start.17) | collective-permute-done | bytes 81952 | tf_op jit(solution)/shard_map/ppermute | solution.py:526
  80.4 3.0 %shard_map.122 = (f32[32,64,128]{2,1,0:T(8,128)S(1)}, f32[2,64,128]{2,1,0:T(8,128)S(1)}, f32[2,64,128]{2,1,0:T(8,128)S(1)}) custom-call(s32[128]{0:T(128)S(1)} %and_select_fusion.row_ref, f32[128,128]{1,0:T(8,128)S(1)} %get-tuple-element.63.value_ref, s32[128,128]{1,0:T(8,128)S(1)} %get-tuple-element.49.col_ref, ...), custom_call_target="tpu_custom_call", output_to_operand_aliasing={{0}: (4, {})} | custom-call | flops 536870912 | bytes 1048576 | tf_op jit(solution)/shard_map/pallas_call | solution.py:510
  83.5 2.1 %collective-permute-start.11 = (f32[2,64,128]{2,1,0:T(8,128)S(1)}, f32[2,64,128]{2,1,0:T(8,128)S(1)}, u32[]{:S(2)}, u32[]{:S(2)}) collective-permute-start(f32[2,64,128]{2,1,0:T(8,128)S(1)} %get-tuple-element.66), channel_id=1, source_target_pairs={{4,8},{12,16},{20,24},{28,0},{8,4},{16,12},{24,20},{0,28},{5,9},{1... | collective-permute-start | bytes 196616 | tf_op jit(solution)/shard_map/ppermute | solution.py:572
  85.6 2.6 %collective-permute-done.11.far_ref = f32[2,64,128]{2,1,0:T(8,128)S(1)} collective-permute-done((f32[2,64,128]{2,1,0:T(8,128)S(1)}, f32[2,64,128]{2,1,0:T(8,128)S(1)}, u32[]{:S(2)}, u32[]{:S(2)}) %collective-permute-start.11) | collective-permute-done | bytes 65568 | tf_op jit(solution)/shard_map/ppermute | solution.py:572
  88.2 1.0 collective-permute-start.12
  89.2 3.5 %collective-permute-start.13 = (f32[36,2,128]{2,1,0:T(2,128)S(1)}, f32[36,2,128]{2,1,0:T(2,128)S(1)}, u32[]{:S(2)}, u32[]{:S(2)}) collective-permute-start(f32[36,2,128]{2,1,0:T(2,128)S(1)} %get-tuple-element.68), channel_id=1, source_target_pairs={{1,2},{3,0},{2,1},{0,3},{5,6},{7,4},{6,5},{4,7},{9,10},{11,8},{10,... | collective-permute-start | bytes 110600 | tf_op jit(solution)/shard_map/ppermute | solution.py:577
  92.8 2.2 %collective-permute-done.13.across_ref = f32[36,2,128]{2,1,0:T(2,128)S(1)} collective-permute-done((f32[36,2,128]{2,1,0:T(2,128)S(1)}, f32[36,2,128]{2,1,0:T(2,128)S(1)}, u32[]{:S(2)}, u32[]{:S(2)}) %collective-permute-start.13) | collective-permute-done | bytes 36896 | tf_op jit(solution)/shard_map/ppermute | solution.py:577
  95.0 7.2 %shard_map.124 = (f32[128,128]{1,0:T(8,128)S(1)}, f32[32,64,128]{2,1,0:T(8,128)S(1)}) custom-call(s32[128]{0:T(128)S(1)} %and_select_fusion.row_ref, f32[1,128]{1,0:T(1,128)S(1)} %bitcast.7, f32[32,64,128]{2,1,0:T(8,128)S(1)} %get-tuple-element.64.g_ref.rest_0_, f32[2,64,128]{2,1,0:T(8,128)S(1)} %collective-permute-done.10.near_ref, ...), custom_call_target="tpu_custom_call" | custom-call | flops 536870912 | bytes 1048576 | tf_op jit(solution)/shard_map/pallas_call | solution.py:510
  102.2 8.6 %shard_map.130 = (f32[128,128]{1,0:T(8,128)S(1)}, f32[20,8,128]{2,1,0:T(8,128)S(1)}, f32[20,8,128]{2,1,0:T(8,128)S(1)}) custom-call(f32[128,128]{1,0:T(8,128)S(1)} %get-tuple-element.69.image_ref, f32[128,128]{1,0:T(8,128)S(1)} %get-tuple-element.56.weight_ref, f32[40,8,128]{2,1,0:T(8,128)S(1)} %get-tuple-element.57.prior_ref, ...), custom_call_target="tpu_custom_call" | custom-call | flops 5368709120 | bytes 1048576 | tf_op jit(solution)/shard_map/pallas_call | solution.py:510
  110.8 1.3 collective-permute-done.24.two_ref
  112.1 0.5 collective-permute-start.25
  112.6 3.6 %collective-permute-done.25.two_ref = f32[10,8,128]{2,1,0:T(8,128)S(1)} collective-permute-done((f32[10,8,128]{2,1,0:T(8,128)S(1)}, f32[10,8,128]{2,1,0:T(8,128)S(1)}, u32[]{:S(2)}, u32[]{:S(2)}) %collective-permute-start.25) | collective-permute-done | bytes 40992 | tf_op jit(solution)/shard_map/ppermute | solution.py:526
  116.2 1.9 %collective-permute-start.26 = (f32[5,8,128]{2,1,0:T(8,128)S(1)}, f32[5,8,128]{2,1,0:T(8,128)S(1)}, u32[]{:S(2)}, u32[]{:S(2)}) collective-permute-start(f32[5,8,128]{2,1,0:T(8,128)S(1)} %get-tuple-element.89), channel_id=1, source_target_pairs={{0,16},{4,20},{8,24},{12,28},{16,0},{20,4},{24,8},{28,12},{1,17},{... | collective-permute-start | bytes 61448 | tf_op jit(solution)/shard_map/ppermute | solution.py:526
  118.1 3.0 %shard_map.131 = (f32[32,64,128]{2,1,0:T(8,128)S(1)}, f32[1,64,128]{2,1,0:T(8,128)S(1)}, f32[1,64,128]{2,1,0:T(8,128)S(1)}) custom-call(s32[128]{0:T(128)S(1)} %and_select_fusion.row_ref, f32[128,128]{1,0:T(8,128)S(1)} %get-tuple-element.74.value_ref, s32[128,128]{1,0:T(8,128)S(1)} %get-tuple-element.49.col_ref, ...), custom_call_target="tpu_custom_call", output_to_operand_aliasing={{0}: (4, {})} | custom-call | flops 536870912 | bytes 1048576 | tf_op jit(solution)/shard_map/pallas_call | solution.py:510
  121.1 0.5 collective-permute-start.21
  121.7 3.8 %collective-permute-done.27.two_ref = f32[5,8,128]{2,1,0:T(8,128)S(1)} collective-permute-done((f32[5,8,128]{2,1,0:T(8,128)S(1)}, f32[5,8,128]{2,1,0:T(8,128)S(1)}, u32[]{:S(2)}, u32[]{:S(2)}) %collective-permute-start.27) | collective-permute-done | bytes 20512 | tf_op jit(solution)/shard_map/ppermute | solution.py:526
  125.4 1.6 %collective-permute-start.28 = (f32[5,8,128]{2,1,0:T(8,128)S(1)}, f32[5,8,128]{2,1,0:T(8,128)S(1)}, u32[]{:S(2)}, u32[]{:S(2)}) collective-permute-start(f32[5,8,128]{2,1,0:T(8,128)S(1)} %shard_map.136.one_ref), channel_id=1, source_target_pairs={{0,2},{1,3},{2,0},{3,1},{4,6},{5,7},{6,4},{7,5},{8,10},{9,11},{10,... | collective-permute-start | bytes 61448 | tf_op jit(solution)/shard_map/ppermute | solution.py:526
  127.1 2.1 %collective-permute-start.22 = (f32[34,1,128]{2,1,0:T(1,128)S(1)}, f32[34,1,128]{2,1,0:T(1,128)S(1)}, u32[]{:S(2)}, u32[]{:S(2)}) collective-permute-start(f32[34,1,128]{2,1,0:T(1,128)S(1)} %get-tuple-element.78), channel_id=1, source_target_pairs={{0,1},{1,0},{2,3},{3,2},{4,5},{5,4},{6,7},{7,6},{8,9},{9,8},{10,11... | collective-permute-start | bytes 52232 | tf_op jit(solution)/shard_map/ppermute | solution.py:526
  129.2 0.8 collective-permute-start.23
  130.0 0.9 collective-permute-done.22.beside_ref
  130.9 3.8 %collective-permute-done.23.across_ref = f32[34,1,128]{2,1,0:T(1,128)S(1)} collective-permute-done((f32[34,1,128]{2,1,0:T(1,128)S(1)}, f32[34,1,128]{2,1,0:T(1,128)S(1)}, u32[]{:S(2)}, u32[]{:S(2)}) %collective-permute-start.23) | collective-permute-done | bytes 17440 | tf_op jit(solution)/shard_map/ppermute | solution.py:577
  134.7 1.3 shard_map.137
  136.0 10.8 %all_to_all.5.sum_ref = f32[32,8,128]{2,1,0:T(8,128)S(1)} all-to-all(f32[32,8,128]{2,1,0:T(8,128)S(1)} %shard_map.137), channel_id=1, replica_groups=mesh['swath'=8,'chan'=4] {'swath','chan'}, dimensions={0} | all-to-all | bytes 262144 | tf_op jit(solution)/shard_map/all_to_all | solution.py:678
  146.8 1.3 shard_map.138
  (50 shorter events, 1.2 us)
Async XLA Ops:
  1.3 26.6 %copy-start.4 = (s32[16384]{0:T(1024)S(1)}, s32[16384]{0:T(1024)}, u32[]{:S(2)}) copy-start(s32[16384]{0:T(1024)} %param.13) | copy-start | bytes 196612
  1.3 33.2 %copy-start = (bf16[16384,128]{1,0:T(8,128)(2,1)S(1)}, bf16[16384,128]{1,0:T(8,128)(2,1)}, u32[]{:S(2)}) copy-start(bf16[16384,128]{1,0:T(8,128)(2,1)} %jac_ref.5) | copy-start | bytes 12582916
  11.4 38.1 %copy-start.3 = (f32[128]{0:T(128)S(1)}, f32[128]{0:T(128)}, u32[]{:S(2)}) copy-start(f32[128]{0:T(128)} %param.16) | copy-start | bytes 1540
  11.5 1.6 %collective-permute-start.4 = (f32[2,20,8,128]{3,2,1,0:T(8,128)S(1)}, f32[2,20,8,128]{3,2,1,0:T(8,128)S(1)}, u32[]{:S(2)}, u32[]{:S(2)}) collective-permute-start(f32[2,20,8,128]{3,2,1,0:T(8,128)S(1)} %get-tuple-element.59), channel_id=1, source_target_pairs={{0,4},{4,0},{8,12},{12,8},{16,20},{20,16},{24,28},{28,24},{1,5},{5... | collective-permute-start | bytes 491528 | tf_op jit(solution)/shard_map/ppermute | solution.py:526
  13.1 7.3 %collective-permute-start.5 = (f32[2,20,8,128]{3,2,1,0:T(8,128)S(1)}, f32[2,20,8,128]{3,2,1,0:T(8,128)S(1)}, u32[]{:S(2)}, u32[]{:S(2)}) collective-permute-start(f32[2,20,8,128]{3,2,1,0:T(8,128)S(1)} %shard_map.116.one_ref), channel_id=1, source_target_pairs={{0,8},{4,12},{8,0},{12,4},{16,24},{20,28},{24,16},{28,20},{1,9},{5... | collective-permute-start | bytes 491528 | tf_op jit(solution)/shard_map/ppermute | solution.py:526
  20.4 5.7 %collective-permute-start.6 = (f32[2,20,8,128]{3,2,1,0:T(8,128)S(1)}, f32[2,20,8,128]{3,2,1,0:T(8,128)S(1)}, u32[]{:S(2)}, u32[]{:S(2)}) collective-permute-start(f32[2,20,8,128]{3,2,1,0:T(8,128)S(1)} %shard_map.117.one_ref), channel_id=1, source_target_pairs={{0,16},{4,20},{8,24},{12,28},{16,0},{20,4},{24,8},{28,12},{1,17},{... | collective-permute-start | bytes 491528 | tf_op jit(solution)/shard_map/ppermute | solution.py:526
  26.2 5.4 %collective-permute-start.7 = (f32[2,20,8,128]{3,2,1,0:T(8,128)S(1)}, f32[2,20,8,128]{3,2,1,0:T(8,128)S(1)}, u32[]{:S(2)}, u32[]{:S(2)}) collective-permute-start(f32[2,20,8,128]{3,2,1,0:T(8,128)S(1)} %shard_map.118.one_ref), channel_id=1, source_target_pairs={{0,1},{1,0},{2,3},{3,2},{4,5},{5,4},{6,7},{7,6},{8,9},{9,8},{10,11... | collective-permute-start | bytes 491528 | tf_op jit(solution)/shard_map/ppermute | solution.py:526
  31.6 12.4 %collective-permute-start.8 = (f32[2,20,8,128]{3,2,1,0:T(8,128)S(1)}, f32[2,20,8,128]{3,2,1,0:T(8,128)S(1)}, u32[]{:S(2)}, u32[]{:S(2)}) collective-permute-start(f32[2,20,8,128]{3,2,1,0:T(8,128)S(1)} %shard_map.119.one_ref), channel_id=1, source_target_pairs={{0,2},{1,3},{2,0},{3,1},{4,6},{5,7},{6,4},{7,5},{8,10},{9,11},{10,... | collective-permute-start | bytes 491528 | tf_op jit(solution)/shard_map/ppermute | solution.py:526
  37.5 2.8 %collective-permute-start = (f32[2,64,128]{2,1,0:T(8,128)S(1)}, f32[2,64,128]{2,1,0:T(8,128)S(1)}, u32[]{:S(2)}, u32[]{:S(2)}) collective-permute-start(f32[2,64,128]{2,1,0:T(8,128)S(1)} %get-tuple-element.51), channel_id=1, source_target_pairs={{0,4},{4,0},{8,12},{12,8},{16,20},{20,16},{24,28},{28,24},{1,5},{5... | collective-permute-start | bytes 196616 | tf_op jit(solution)/shard_map/ppermute | solution.py:526
  37.6 4.7 %collective-permute-start.1 = (f32[2,64,128]{2,1,0:T(8,128)S(1)}, f32[2,64,128]{2,1,0:T(8,128)S(1)}, u32[]{:S(2)}, u32[]{:S(2)}) collective-permute-start(f32[2,64,128]{2,1,0:T(8,128)S(1)} %get-tuple-element.52), channel_id=1, source_target_pairs={{4,8},{12,16},{20,24},{28,0},{8,4},{16,12},{24,20},{0,28},{5,9},{1... | collective-permute-start | bytes 196616 | tf_op jit(solution)/shard_map/ppermute | solution.py:572
  42.3 4.0 %collective-permute-start.2 = (f32[36,2,128]{2,1,0:T(2,128)S(1)}, f32[36,2,128]{2,1,0:T(2,128)S(1)}, u32[]{:S(2)}, u32[]{:S(2)}) collective-permute-start(f32[36,2,128]{2,1,0:T(2,128)S(1)} %get-tuple-element.53), channel_id=1, source_target_pairs={{0,1},{1,0},{2,3},{3,2},{4,5},{5,4},{6,7},{7,6},{8,9},{9,8},{10,11... | collective-permute-start | bytes 110600 | tf_op jit(solution)/shard_map/ppermute | solution.py:526
  43.8 5.8 %collective-permute-start.3 = (f32[36,2,128]{2,1,0:T(2,128)S(1)}, f32[36,2,128]{2,1,0:T(2,128)S(1)}, u32[]{:S(2)}, u32[]{:S(2)}) collective-permute-start(f32[36,2,128]{2,1,0:T(2,128)S(1)} %get-tuple-element.54), channel_id=1, source_target_pairs={{1,2},{3,0},{2,1},{0,3},{5,6},{7,4},{6,5},{4,7},{9,10},{11,8},{10,... | collective-permute-start | bytes 110600 | tf_op jit(solution)/shard_map/ppermute | solution.py:577
  44.0 12.8 %collective-permute-start.9 = (f32[20,8,128]{2,1,0:T(8,128)S(1)}, f32[20,8,128]{2,1,0:T(8,128)S(1)}, u32[]{:S(2)}, u32[]{:S(2)}) collective-permute-start(f32[20,8,128]{2,1,0:T(8,128)S(1)} %get-tuple-element.60.mine_ref.zb_ref.zm_ref), channel_id=1, source_target_pairs={{0,4},{4,0},{8,12},{12,8},{16,20},{20,16},{24,28},{28,24},{1,5},{5... | collective-permute-start | bytes 245768 | tf_op jit(solution)/shard_map/ppermute | solution.py:526
  56.8 23.6 %copy-start.1 = (bf16[16384,128]{1,0:T(8,128)(2,1)S(1)}, bf16[16384,128]{1,0:T(8,128)(2,1)}, u32[]{:S(2)}) copy-start(bf16[16384,128]{1,0:T(8,128)(2,1)} %jac_ref.5) | copy-start | bytes 12582916
  65.3 1.3 collective-permute-start.14
  66.7 4.6 %collective-permute-start.15 = (f32[20,8,128]{2,1,0:T(8,128)S(1)}, f32[20,8,128]{2,1,0:T(8,128)S(1)}, u32[]{:S(2)}, u32[]{:S(2)}) collective-permute-start(f32[20,8,128]{2,1,0:T(8,128)S(1)} %shard_map.125.one_ref), channel_id=1, source_target_pairs={{0,8},{4,12},{8,0},{12,4},{16,24},{20,28},{24,16},{28,20},{1,9},{5... | collective-permute-start | bytes 245768 | tf_op jit(solution)/shard_map/ppermute | solution.py:526
  71.3 4.5 %collective-permute-start.16 = (f32[20,8,128]{2,1,0:T(8,128)S(1)}, f32[20,8,128]{2,1,0:T(8,128)S(1)}, u32[]{:S(2)}, u32[]{:S(2)}) collective-permute-start(f32[20,8,128]{2,1,0:T(8,128)S(1)} %shard_map.126.one_ref), channel_id=1, source_target_pairs={{0,16},{4,20},{8,24},{12,28},{16,0},{20,4},{24,8},{28,12},{1,17},{... | collective-permute-start | bytes 245768 | tf_op jit(solution)/shard_map/ppermute | solution.py:526
  75.8 4.5 %collective-permute-start.17 = (f32[20,8,128]{2,1,0:T(8,128)S(1)}, f32[20,8,128]{2,1,0:T(8,128)S(1)}, u32[]{:S(2)}, u32[]{:S(2)}) collective-permute-start(f32[20,8,128]{2,1,0:T(8,128)S(1)} %shard_map.127.one_ref), channel_id=1, source_target_pairs={{0,1},{1,0},{2,3},{3,2},{4,5},{5,4},{6,7},{7,6},{8,9},{9,8},{10,11... | collective-permute-start | bytes 245768 | tf_op jit(solution)/shard_map/ppermute | solution.py:526
  80.3 12.4 %collective-permute-start.18 = (f32[20,8,128]{2,1,0:T(8,128)S(1)}, f32[20,8,128]{2,1,0:T(8,128)S(1)}, u32[]{:S(2)}, u32[]{:S(2)}) collective-permute-start(f32[20,8,128]{2,1,0:T(8,128)S(1)} %shard_map.128.one_ref), channel_id=1, source_target_pairs={{0,2},{1,3},{2,0},{3,1},{4,6},{5,7},{6,4},{7,5},{8,10},{9,11},{10,... | collective-permute-start | bytes 245768 | tf_op jit(solution)/shard_map/ppermute | solution.py:526
  83.4 2.2 %collective-permute-start.10 = (f32[2,64,128]{2,1,0:T(8,128)S(1)}, f32[2,64,128]{2,1,0:T(8,128)S(1)}, u32[]{:S(2)}, u32[]{:S(2)}) collective-permute-start(f32[2,64,128]{2,1,0:T(8,128)S(1)} %get-tuple-element.65), channel_id=1, source_target_pairs={{0,4},{4,0},{8,12},{12,8},{16,20},{20,16},{24,28},{28,24},{1,5},{5... | collective-permute-start | bytes 196616 | tf_op jit(solution)/shard_map/ppermute | solution.py:526
  83.5 4.7 %collective-permute-start.11 = (f32[2,64,128]{2,1,0:T(8,128)S(1)}, f32[2,64,128]{2,1,0:T(8,128)S(1)}, u32[]{:S(2)}, u32[]{:S(2)}) collective-permute-start(f32[2,64,128]{2,1,0:T(8,128)S(1)} %get-tuple-element.66), channel_id=1, source_target_pairs={{4,8},{12,16},{20,24},{28,0},{8,4},{16,12},{24,20},{0,28},{5,9},{1... | collective-permute-start | bytes 196616 | tf_op jit(solution)/shard_map/ppermute | solution.py:572
  88.2 4.6 %collective-permute-start.12 = (f32[36,2,128]{2,1,0:T(2,128)S(1)}, f32[36,2,128]{2,1,0:T(2,128)S(1)}, u32[]{:S(2)}, u32[]{:S(2)}) collective-permute-start(f32[36,2,128]{2,1,0:T(2,128)S(1)} %get-tuple-element.67), channel_id=1, source_target_pairs={{0,1},{1,0},{2,3},{3,2},{4,5},{5,4},{6,7},{7,6},{8,9},{9,8},{10,11... | collective-permute-start | bytes 110600 | tf_op jit(solution)/shard_map/ppermute | solution.py:526
  89.2 5.8 %collective-permute-start.13 = (f32[36,2,128]{2,1,0:T(2,128)S(1)}, f32[36,2,128]{2,1,0:T(2,128)S(1)}, u32[]{:S(2)}, u32[]{:S(2)}) collective-permute-start(f32[36,2,128]{2,1,0:T(2,128)S(1)} %get-tuple-element.68), channel_id=1, source_target_pairs={{1,2},{3,0},{2,1},{0,3},{5,6},{7,4},{6,5},{4,7},{9,10},{11,8},{10,... | collective-permute-start | bytes 110600 | tf_op jit(solution)/shard_map/ppermute | solution.py:577
  92.7 9.5 %collective-permute-start.19 = (f32[20,8,128]{2,1,0:T(8,128)S(1)}, f32[20,8,128]{2,1,0:T(8,128)S(1)}, u32[]{:S(2)}, u32[]{:S(2)}) collective-permute-start(f32[20,8,128]{2,1,0:T(8,128)S(1)} %get-tuple-element.73.mine_ref.ub_ref.um_ref), channel_id=1, source_target_pairs={{0,4},{4,0},{8,12},{12,8},{16,20},{20,16},{24,28},{28,24},{1,5},{5... | collective-permute-start | bytes 245768 | tf_op jit(solution)/shard_map/ppermute | solution.py:526
  102.2 15.9 %copy-start.2 = (bf16[16384,128]{1,0:T(8,128)(2,1)S(1)}, bf16[16384,128]{1,0:T(8,128)(2,1)}, u32[]{:S(2)}) copy-start(bf16[16384,128]{1,0:T(8,128)(2,1)} %jac_ref.5) | copy-start | bytes 12582916
  110.7 1.3 collective-permute-start.24
  112.1 4.1 %collective-permute-start.25 = (f32[10,8,128]{2,1,0:T(8,128)S(1)}, f32[10,8,128]{2,1,0:T(8,128)S(1)}, u32[]{:S(2)}, u32[]{:S(2)}) collective-permute-start(f32[10,8,128]{2,1,0:T(8,128)S(1)} %get-tuple-element.87), channel_id=1, source_target_pairs={{0,8},{4,12},{8,0},{12,4},{16,24},{20,28},{24,16},{28,20},{1,9},{5... | collective-permute-start | bytes 122888 | tf_op jit(solution)/shard_map/ppermute | solution.py:526
  116.2 5.4 %collective-permute-start.26 = (f32[5,8,128]{2,1,0:T(8,128)S(1)}, f32[5,8,128]{2,1,0:T(8,128)S(1)}, u32[]{:S(2)}, u32[]{:S(2)}) collective-permute-start(f32[5,8,128]{2,1,0:T(8,128)S(1)} %get-tuple-element.89), channel_id=1, source_target_pairs={{0,16},{4,20},{8,24},{12,28},{16,0},{20,4},{24,8},{28,12},{1,17},{... | collective-permute-start | bytes 61448 | tf_op jit(solution)/shard_map/ppermute | solution.py:526
  121.0 6.0 %collective-permute-start.20 = (f32[1,64,128]{2,1,0:T(8,128)S(1)}, f32[1,64,128]{2,1,0:T(8,128)S(1)}, u32[]{:S(2)}, u32[]{:S(2)}) collective-permute-start(f32[1,64,128]{2,1,0:T(8,128)S(1)} %get-tuple-element.76), channel_id=1, source_target_pairs={{0,4},{4,0},{8,12},{12,8},{16,20},{20,16},{24,28},{28,24},{1,5},{5... | collective-permute-start | bytes 98312 | tf_op jit(solution)/shard_map/ppermute | solution.py:526
  121.1 5.9 %collective-permute-start.21 = (f32[1,64,128]{2,1,0:T(8,128)S(1)}, f32[1,64,128]{2,1,0:T(8,128)S(1)}, u32[]{:S(2)}, u32[]{:S(2)}) collective-permute-start(f32[1,64,128]{2,1,0:T(8,128)S(1)} %get-tuple-element.77), channel_id=1, source_target_pairs={{4,8},{12,16},{20,24},{28,0},{8,4},{16,12},{24,20},{0,28},{5,9},{1... | collective-permute-start | bytes 98312 | tf_op jit(solution)/shard_map/ppermute | solution.py:572
  121.6 3.8 %collective-permute-start.27 = (f32[5,8,128]{2,1,0:T(8,128)S(1)}, f32[5,8,128]{2,1,0:T(8,128)S(1)}, u32[]{:S(2)}, u32[]{:S(2)}) collective-permute-start(f32[5,8,128]{2,1,0:T(8,128)S(1)} %shard_map.135.one_ref), channel_id=1, source_target_pairs={{0,1},{1,0},{2,3},{3,2},{4,5},{5,4},{6,7},{7,6},{8,9},{9,8},{10,11... | collective-permute-start | bytes 61448 | tf_op jit(solution)/shard_map/ppermute | solution.py:526
  125.4 9.3 %collective-permute-start.28 = (f32[5,8,128]{2,1,0:T(8,128)S(1)}, f32[5,8,128]{2,1,0:T(8,128)S(1)}, u32[]{:S(2)}, u32[]{:S(2)}) collective-permute-start(f32[5,8,128]{2,1,0:T(8,128)S(1)} %shard_map.136.one_ref), channel_id=1, source_target_pairs={{0,2},{1,3},{2,0},{3,1},{4,6},{5,7},{6,4},{7,5},{8,10},{9,11},{10,... | collective-permute-start | bytes 61448 | tf_op jit(solution)/shard_map/ppermute | solution.py:526
  127.1 3.8 %collective-permute-start.22 = (f32[34,1,128]{2,1,0:T(1,128)S(1)}, f32[34,1,128]{2,1,0:T(1,128)S(1)}, u32[]{:S(2)}, u32[]{:S(2)}) collective-permute-start(f32[34,1,128]{2,1,0:T(1,128)S(1)} %get-tuple-element.78), channel_id=1, source_target_pairs={{0,1},{1,0},{2,3},{3,2},{4,5},{5,4},{6,7},{7,6},{8,9},{9,8},{10,11... | collective-permute-start | bytes 52232 | tf_op jit(solution)/shard_map/ppermute | solution.py:526
  129.2 5.5 %collective-permute-start.23 = (f32[34,1,128]{2,1,0:T(1,128)S(1)}, f32[34,1,128]{2,1,0:T(1,128)S(1)}, u32[]{:S(2)}, u32[]{:S(2)}) collective-permute-start(f32[34,1,128]{2,1,0:T(1,128)S(1)} %get-tuple-element.79), channel_id=1, source_target_pairs={{1,2},{3,0},{2,1},{0,3},{5,6},{7,4},{6,5},{4,7},{9,10},{11,8},{10,... | collective-permute-start | bytes 52232 | tf_op jit(solution)/shard_map/ppermute | solution.py:577
where the time goes:
time: 148 us
  Pallas kernels  53.6 us (36%)
  waiting for transfers between devices  50.5 us (34%)
  starting transfers between devices  31.5 us (21%)
  blocking collectives  10.8 us (7%)
  between operations  1.57 us (1%)
    pallas_call x27, Pallas kernels, place_call(): pl.pallas_call(kernel, out_shape=shapes, in_specs=specs, out_specs=[VMEM]...  53.6 us
    ppermute x23, waiting for transfers between devices, trade(): return lax.ppermute(value, axis, [(i, i ^ mask) for i in range(size)])  36.7 us
    ppermute x23, starting transfers between devices, trade(): return lax.ppermute(value, axis, [(i, i ^ mask) for i in range(size)])  21.8 us
    all_to_all x1, blocking collectives, body(): sums = lax.all_to_all(sums, ('swath', 'chan'), 0, 0)  10.8 us
    ppermute x3, waiting for transfers between devices, halos(): across = lax.ppermute(across, 'chan', pairs + [(j, i) for i, j in pairs])  9.27 us
    ppermute x3, starting transfers between devices, halos(): far = lax.ppermute(far, 'swath', pairs + [(j, i) for i, j in pairs])  5.27 us
    ppermute x3, waiting for transfers between devices, halos(): far = lax.ppermute(far, 'swath', pairs + [(j, i) for i, j in pairs])  4.52 us
    ppermute x3, starting transfers between devices, halos(): across = lax.ppermute(across, 'chan', pairs + [(j, i) for i, j in pairs])  4.41 us
  transfers between devices with their start and end apart: 29, of which 18 were waited for; matrix products, arithmetic and copies ran while one was open for 0% of the time, Pallas kernels for 16%

commit v1 on v0

--- a/solution.py
+++ b/solution.py
@@ -206,7 +206,7 @@
         return following
 
     last = lines // GROUP - 1
-    tell(last, lax.fori_loop(1, last + 1, step, look(0)))
+    tell(last, lax.fori_loop(1, last + 1, step, look(0), unroll=last))
     put_table(table_ref, acc_ref, blocks, lambda unit: prior_ref[unit] * full_ref[unit])
     give_halves(table_ref, keep_ref, send_ref)
 
@@ -269,7 +269,7 @@
             out_ref[row] += got[:LON_DEV] + got[LON_DEV:]
         return 0
 
-    lax.fori_loop(first, last, step, 0, unroll=UNROLL)
+    lax.fori_loop(first, last, step, 0, unroll=2 * UNROLL)
     if scale != 1.0:
         out_ref[...] = out_ref[...] * scale
     if width:
@@ -454,13 +454,13 @@
         both = state + jnp.sum(one * two, axis=0) * share
         both = jnp.sum(jnp.sum(both, axis=0, keepdims=True), axis=1, keepdims=True)
         sums = jnp.where(lane == k, both, sums)
-    sum_ref[...] = jnp.broadcast_to(sums[None], sum_ref.shape)
+    sum_ref[...] = jnp.broadcast_to(sums[:1][None], sum_ref.shape)
 
 
 def final_kernel(
     sum_ref, z_ref, w_ref, zm_ref, zo_ref, um_ref, uo_ref, x_ref, xb_ref, norm_ref
 ):
-    sums = jnp.sum(sum_ref[...], axis=0)[:1]
+    sums = jnp.sum(sum_ref[...], axis=0)
     lane = lax.broadcasted_iota(jnp.int32, (1, LANES), 1)
     rr, rz, zw, rw, wu, ww, uv, rv, wv, vv = (
         jnp.sum(jnp.where(lane == k, sums, 0.0), axis=1, keepdims=True) for k in range(10)
@@ -671,7 +671,7 @@
     parts, cuts = chips_scatter(mine, got)
     copies = bands * sectors * parts[0].shape[0] // units
     gram = call(
-        functools.partial(gram_kernel, 1.0 / copies, cuts), [((bands * sectors, 8, LANES), F32)],
+        functools.partial(gram_kernel, 1.0 / copies, cuts), [((bands * sectors, 1, LANES), F32)],
         [pltpu.VMEM((LAT_DEV + 2, wide, LEV), F32)], 1 << 22,
     )
     sums = gram(smooth, *halos(*g2), z, w, rb, zb, wb, ub, *parts)[0]

time: 148 us -> 141 us (0.953)
  Pallas kernels: 53.6 us -> 47.3 us
    pallas_call x27, Pallas kernels: 53.6 us -> 47.3 us  [place_call(): pl.pallas_call(kernel, out_shape=shapes, in_specs=specs, out_specs=[VMEM]...]
where the time goes in v1:
time: 141 us
  waiting for transfers between devices  51.1 us (36%)
  Pallas kernels  47.3 us (34%)
  starting transfers between devices  30.9 us (22%)
  blocking collectives  9.54 us (7%)
  between operations  1.57 us (1%)
    pallas_call x27, Pallas kernels, place_call(): pl.pallas_call(kernel, out_shape=shapes, in_specs=specs, out_specs=[VMEM]...  47.3 us
    ppermute x23, waiting for transfers between devices, trade(): return lax.ppermute(value, axis, [(i, i ^ mask) for i in range(size)])  37.1 us
    ppermute x23, starting transfers between devices, trade(): return lax.ppermute(value, axis, [(i, i ^ mask) for i in range(size)])  21.6 us
    all_to_all x1, blocking collectives, body(): sums = lax.all_to_all(sums, ('swath', 'chan'), 0, 0)  9.54 us
    ppermute x3, waiting for transfers between devices, halos(): across = lax.ppermute(across, 'chan', pairs + [(j, i) for i, j in pairs])  9.17 us
    ppermute x3, starting transfers between devices, halos(): far = lax.ppermute(far, 'swath', pairs + [(j, i) for i, j in pairs])  4.93 us
    ppermute x3, waiting for transfers between devices, halos(): far = lax.ppermute(far, 'swath', pairs + [(j, i) for i, j in pairs])  4.91 us
    ppermute x3, starting transfers between devices, halos(): across = lax.ppermute(across, 'chan', pairs + [(j, i) for i, j in pairs])  4.42 us
  transfers between devices with their start and end apart: 29, of which 18 were waited for; matrix products, arithmetic and copies ran while one was open for 0% of the time, Pallas kernels for 16%

profile of v1, /device:TPU:0, one launch (start us, length us, event | category | flops | bytes accessed | tf_op | source)
XLA Modules:
  0.0 140.7 jit_solution(9596946022571943802)
XLA Ops:
  1.3 10.2 %shard_map.112 = (f32[128,128]{1,0:T(8,128)S(1)}, f32[128,128]{1,0:T(8,128)S(1)}, f32[2,20,8,128]{3,2,1,0:T(8,128)S(1)}, f32[2,20,8,128]{3,2,1,0:T(8,128)S(1)}, ...) custom-call(s32[1,1]{1,0:T(1,128)S(6)} %copy.16.count_ref, ...), custom_call_target="tpu_custom_call" | custom-call | flops 5368709120 | bytes 1048576 | tf_op jit(solution)/shard_map/pallas_call | solution.py:510
  11.5 0.5 collective-permute-start.4
  12.0 1.0 collective-permute-done.4.two_ref
  13.1 2.9 %collective-permute-start.5 = (f32[2,20,8,128]{3,2,1,0:T(8,128)S(1)}, f32[2,20,8,128]{3,2,1,0:T(8,128)S(1)}, u32[]{:S(2)}, u32[]{:S(2)}) collective-permute-start(f32[2,20,8,128]{3,2,1,0:T(8,128)S(1)} %shard_map.116.one_ref), channel_id=1, source_target_pairs={{0,8},{4,12},{8,0},{12,4},{16,24},{20,28},{24,16},{28,20},{1,9},{5... | collective-permute-start | bytes 491528 | tf_op jit(solution)/shard_map/ppermute | solution.py:526
  16.0 4.5 %collective-permute-done.5.two_ref = f32[2,20,8,128]{3,2,1,0:T(8,128)S(1)} collective-permute-done((f32[2,20,8,128]{3,2,1,0:T(8,128)S(1)}, f32[2,20,8,128]{3,2,1,0:T(8,128)S(1)}, u32[]{:S(2)}, u32[]{:S(2)}) %collective-permute-start.5) | collective-permute-done | bytes 163872 | tf_op jit(solution)/shard_map/ppermute | solution.py:526
  20.5 1.8 %collective-permute-start.6 = (f32[2,20,8,128]{3,2,1,0:T(8,128)S(1)}, f32[2,20,8,128]{3,2,1,0:T(8,128)S(1)}, u32[]{:S(2)}, u32[]{:S(2)}) collective-permute-start(f32[2,20,8,128]{3,2,1,0:T(8,128)S(1)} %shard_map.117.one_ref), channel_id=1, source_target_pairs={{0,16},{4,20},{8,24},{12,28},{16,0},{20,4},{24,8},{28,12},{1,17},{... | collective-permute-start | bytes 491528 | tf_op jit(solution)/shard_map/ppermute | solution.py:526
  22.3 3.9 %collective-permute-done.6.two_ref = f32[2,20,8,128]{3,2,1,0:T(8,128)S(1)} collective-permute-done((f32[2,20,8,128]{3,2,1,0:T(8,128)S(1)}, f32[2,20,8,128]{3,2,1,0:T(8,128)S(1)}, u32[]{:S(2)}, u32[]{:S(2)}) %collective-permute-start.6) | collective-permute-done | bytes 163872 | tf_op jit(solution)/shard_map/ppermute | solution.py:526
  26.3 1.6 %collective-permute-start.7 = (f32[2,20,8,128]{3,2,1,0:T(8,128)S(1)}, f32[2,20,8,128]{3,2,1,0:T(8,128)S(1)}, u32[]{:S(2)}, u32[]{:S(2)}) collective-permute-start(f32[2,20,8,128]{3,2,1,0:T(8,128)S(1)} %shard_map.118.one_ref), channel_id=1, source_target_pairs={{0,1},{1,0},{2,3},{3,2},{4,5},{5,4},{6,7},{7,6},{8,9},{9,8},{10,11... | collective-permute-start | bytes 491528 | tf_op jit(solution)/shard_map/ppermute | solution.py:526
  28.0 3.6 %collective-permute-done.7.two_ref = f32[2,20,8,128]{3,2,1,0:T(8,128)S(1)} collective-permute-done((f32[2,20,8,128]{3,2,1,0:T(8,128)S(1)}, f32[2,20,8,128]{3,2,1,0:T(8,128)S(1)}, u32[]{:S(2)}, u32[]{:S(2)}) %collective-permute-start.7) | collective-permute-done | bytes 163872 | tf_op jit(solution)/shard_map/ppermute | solution.py:526
  31.7 2.8 %collective-permute-start.8 = (f32[2,20,8,128]{3,2,1,0:T(8,128)S(1)}, f32[2,20,8,128]{3,2,1,0:T(8,128)S(1)}, u32[]{:S(2)}, u32[]{:S(2)}) collective-permute-start(f32[2,20,8,128]{3,2,1,0:T(8,128)S(1)} %shard_map.119.one_ref), channel_id=1, source_target_pairs={{0,2},{1,3},{2,0},{3,1},{4,6},{5,7},{6,4},{7,5},{8,10},{9,11},{10,... | collective-permute-start | bytes 491528 | tf_op jit(solution)/shard_map/ppermute | solution.py:526
  34.5 2.4 %shard_map.113 = (f32[32,64,128]{2,1,0:T(8,128)S(1)}, f32[2,64,128]{2,1,0:T(8,128)S(1)}, f32[2,64,128]{2,1,0:T(8,128)S(1)}) custom-call(s32[128]{0:T(128)S(1)} %and_select_fusion.row_ref, f32[128,128]{1,0:T(8,128)S(1)} %get-tuple-element.48.value_ref, s32[128,128]{1,0:T(8,128)S(1)} %get-tuple-element.49.col_ref, bf16[16384,128]{1,0:T(8,128)(2,1)S(1)} %copy-done), custom_call_target="tpu_custom_call" | custom-call | flops 536870912 | bytes 1048576 | tf_op jit(solution)/shard_map/pallas_call | solution.py:510
  37.0 2.4 %collective-permute-start.1 = (f32[2,64,128]{2,1,0:T(8,128)S(1)}, f32[2,64,128]{2,1,0:T(8,128)S(1)}, u32[]{:S(2)}, u32[]{:S(2)}) collective-permute-start(f32[2,64,128]{2,1,0:T(8,128)S(1)} %get-tuple-element.52), channel_id=1, source_target_pairs={{4,8},{12,16},{20,24},{28,0},{8,4},{16,12},{24,20},{0,28},{5,9},{1... | collective-permute-start | bytes 196616 | tf_op jit(solution)/shard_map/ppermute | solution.py:572
  39.5 2.3 %collective-permute-done.1.far_ref = f32[2,64,128]{2,1,0:T(8,128)S(1)} collective-permute-done((f32[2,64,128]{2,1,0:T(8,128)S(1)}, f32[2,64,128]{2,1,0:T(8,128)S(1)}, u32[]{:S(2)}, u32[]{:S(2)}) %collective-permute-start.1) | collective-permute-done | bytes 65568 | tf_op jit(solution)/shard_map/ppermute | solution.py:572
  41.8 1.4 %collective-permute-start.2 = (f32[36,2,128]{2,1,0:T(2,128)S(1)}, f32[36,2,128]{2,1,0:T(2,128)S(1)}, u32[]{:S(2)}, u32[]{:S(2)}) collective-permute-start(f32[36,2,128]{2,1,0:T(2,128)S(1)} %get-tuple-element.53), channel_id=1, source_target_pairs={{0,1},{1,0},{2,3},{3,2},{4,5},{5,4},{6,7},{7,6},{8,9},{9,8},{10,11... | collective-permute-start | bytes 110600 | tf_op jit(solution)/shard_map/ppermute | solution.py:526
  43.2 0.2 collective-permute-start.3
  43.6 2.3 %collective-permute-done.2.beside_ref = f32[36,2,128]{2,1,0:T(2,128)S(1)} collective-permute-done((f32[36,2,128]{2,1,0:T(2,128)S(1)}, f32[36,2,128]{2,1,0:T(2,128)S(1)}, u32[]{:S(2)}, u32[]{:S(2)}) %collective-permute-start.2) | collective-permute-done | bytes 36896 | tf_op jit(solution)/shard_map/ppermute | solution.py:526
  45.9 3.2 %collective-permute-done.3.across_ref = f32[36,2,128]{2,1,0:T(2,128)S(1)} collective-permute-done((f32[36,2,128]{2,1,0:T(2,128)S(1)}, f32[36,2,128]{2,1,0:T(2,128)S(1)}, u32[]{:S(2)}, u32[]{:S(2)}) %collective-permute-start.3) | collective-permute-done | bytes 36896 | tf_op jit(solution)/shard_map/ppermute | solution.py:577
  49.0 7.2 %shard_map.115 = (f32[128,128]{1,0:T(8,128)S(1)}, f32[32,64,128]{2,1,0:T(8,128)S(1)}) custom-call(s32[128]{0:T(128)S(1)} %and_select_fusion.row_ref, f32[1,128]{1,0:T(1,128)S(1)} %bitcast.6, f32[32,64,128]{2,1,0:T(8,128)S(1)} %get-tuple-element.50.g_ref.rest_0_, f32[2,64,128]{2,1,0:T(8,128)S(1)} %collective-permute-done.near_ref, ...), custom_call_target="tpu_custom_call" | custom-call | flops 536870912 | bytes 1048576 | tf_op jit(solution)/shard_map/pallas_call | solution.py:510
  56.2 6.2 %shard_map.121 = (f32[128,128]{1,0:T(8,128)S(1)}, f32[20,8,128]{2,1,0:T(8,128)S(1)}, f32[20,8,128]{2,1,0:T(8,128)S(1)}) custom-call(f32[128,128]{1,0:T(8,128)S(1)} %get-tuple-element.55.image_ref, f32[128,128]{1,0:T(8,128)S(1)} %get-tuple-element.56.weight_ref, f32[40,8,128]{2,1,0:T(8,128)S(1)} %get-tuple-element.57.prior_ref, ...), custom_call_target="tpu_custom_call" | custom-call | flops 5368709120 | bytes 1048576 | tf_op jit(solution)/shard_map/pallas_call | solution.py:510
  62.5 1.3 collective-permute-done.14.two_ref
  63.8 0.8 collective-permute-start.15
  64.6 3.7 %collective-permute-done.15.two_ref = f32[20,8,128]{2,1,0:T(8,128)S(1)} collective-permute-done((f32[20,8,128]{2,1,0:T(8,128)S(1)}, f32[20,8,128]{2,1,0:T(8,128)S(1)}, u32[]{:S(2)}, u32[]{:S(2)}) %collective-permute-start.15) | collective-permute-done | bytes 81952 | tf_op jit(solution)/shard_map/ppermute | solution.py:526
  68.4 1.9 %collective-permute-start.16 = (f32[20,8,128]{2,1,0:T(8,128)S(1)}, f32[20,8,128]{2,1,0:T(8,128)S(1)}, u32[]{:S(2)}, u32[]{:S(2)}) collective-permute-start(f32[20,8,128]{2,1,0:T(8,128)S(1)} %shard_map.126.one_ref), channel_id=1, source_target_pairs={{0,16},{4,20},{8,24},{12,28},{16,0},{20,4},{24,8},{28,12},{1,17},{... | collective-permute-start | bytes 245768 | tf_op jit(solution)/shard_map/ppermute | solution.py:526
  70.2 2.6 %collective-permute-done.16.two_ref = f32[20,8,128]{2,1,0:T(8,128)S(1)} collective-permute-done((f32[20,8,128]{2,1,0:T(8,128)S(1)}, f32[20,8,128]{2,1,0:T(8,128)S(1)}, u32[]{:S(2)}, u32[]{:S(2)}) %collective-permute-start.16) | collective-permute-done | bytes 81952 | tf_op jit(solution)/shard_map/ppermute | solution.py:526
  73.0 4.4 %collective-permute-done.17.two_ref = f32[20,8,128]{2,1,0:T(8,128)S(1)} collective-permute-done((f32[20,8,128]{2,1,0:T(8,128)S(1)}, f32[20,8,128]{2,1,0:T(8,128)S(1)}, u32[]{:S(2)}, u32[]{:S(2)}) %collective-permute-start.17) | collective-permute-done | bytes 81952 | tf_op jit(solution)/shard_map/ppermute | solution.py:526
  77.5 2.4 %shard_map.122 = (f32[32,64,128]{2,1,0:T(8,128)S(1)}, f32[2,64,128]{2,1,0:T(8,128)S(1)}, f32[2,64,128]{2,1,0:T(8,128)S(1)}) custom-call(s32[128]{0:T(128)S(1)} %and_select_fusion.row_ref, f32[128,128]{1,0:T(8,128)S(1)} %get-tuple-element.63.value_ref, s32[128,128]{1,0:T(8,128)S(1)} %get-tuple-element.49.col_ref, ...), custom_call_target="tpu_custom_call", output_to_operand_aliasing={{0}: (4, {})} | custom-call | flops 536870912 | bytes 1048576 | tf_op jit(solution)/shard_map/pallas_call | solution.py:510
  80.0 2.0 %collective-permute-start.11 = (f32[2,64,128]{2,1,0:T(8,128)S(1)}, f32[2,64,128]{2,1,0:T(8,128)S(1)}, u32[]{:S(2)}, u32[]{:S(2)}) collective-permute-start(f32[2,64,128]{2,1,0:T(8,128)S(1)} %get-tuple-element.66), channel_id=1, source_target_pairs={{4,8},{12,16},{20,24},{28,0},{8,4},{16,12},{24,20},{0,28},{5,9},{1... | collective-permute-start | bytes 196616 | tf_op jit(solution)/shard_map/ppermute | solution.py:572
  82.0 2.6 %collective-permute-done.11.far_ref = f32[2,64,128]{2,1,0:T(8,128)S(1)} collective-permute-done((f32[2,64,128]{2,1,0:T(8,128)S(1)}, f32[2,64,128]{2,1,0:T(8,128)S(1)}, u32[]{:S(2)}, u32[]{:S(2)}) %collective-permute-start.11) | collective-permute-done | bytes 65568 | tf_op jit(solution)/shard_map/ppermute | solution.py:572
  84.7 1.0 collective-permute-start.12
  85.7 3.5 %collective-permute-start.13 = (f32[36,2,128]{2,1,0:T(2,128)S(1)}, f32[36,2,128]{2,1,0:T(2,128)S(1)}, u32[]{:S(2)}, u32[]{:S(2)}) collective-permute-start(f32[36,2,128]{2,1,0:T(2,128)S(1)} %get-tuple-element.68), channel_id=1, source_target_pairs={{1,2},{3,0},{2,1},{0,3},{5,6},{7,4},{6,5},{4,7},{9,10},{11,8},{10,... | collective-permute-start | bytes 110600 | tf_op jit(solution)/shard_map/ppermute | solution.py:577
  89.3 2.2 %collective-permute-done.13.across_ref = f32[36,2,128]{2,1,0:T(2,128)S(1)} collective-permute-done((f32[36,2,128]{2,1,0:T(2,128)S(1)}, f32[36,2,128]{2,1,0:T(2,128)S(1)}, u32[]{:S(2)}, u32[]{:S(2)}) %collective-permute-start.13) | collective-permute-done | bytes 36896 | tf_op jit(solution)/shard_map/ppermute | solution.py:577
  91.5 7.3 %shard_map.124 = (f32[128,128]{1,0:T(8,128)S(1)}, f32[32,64,128]{2,1,0:T(8,128)S(1)}) custom-call(s32[128]{0:T(128)S(1)} %and_select_fusion.row_ref, f32[1,128]{1,0:T(1,128)S(1)} %bitcast.7, f32[32,64,128]{2,1,0:T(8,128)S(1)} %get-tuple-element.64.g_ref.rest_0_, f32[2,64,128]{2,1,0:T(8,128)S(1)} %collective-permute-done.10.near_ref, ...), custom_call_target="tpu_custom_call" | custom-call | flops 536870912 | bytes 1048576 | tf_op jit(solution)/shard_map/pallas_call | solution.py:510
  98.9 6.2 %shard_map.130 = (f32[128,128]{1,0:T(8,128)S(1)}, f32[20,8,128]{2,1,0:T(8,128)S(1)}, f32[20,8,128]{2,1,0:T(8,128)S(1)}) custom-call(f32[128,128]{1,0:T(8,128)S(1)} %get-tuple-element.69.image_ref, f32[128,128]{1,0:T(8,128)S(1)} %get-tuple-element.56.weight_ref, f32[40,8,128]{2,1,0:T(8,128)S(1)} %get-tuple-element.57.prior_ref, ...), custom_call_target="tpu_custom_call" | custom-call | flops 5368709120 | bytes 1048576 | tf_op jit(solution)/shard_map/pallas_call | solution.py:510
  105.1 1.3 collective-permute-done.24.two_ref
  106.4 0.5 collective-permute-start.25
  106.9 3.6 %collective-permute-done.25.two_ref = f32[10,8,128]{2,1,0:T(8,128)S(1)} collective-permute-done((f32[10,8,128]{2,1,0:T(8,128)S(1)}, f32[10,8,128]{2,1,0:T(8,128)S(1)}, u32[]{:S(2)}, u32[]{:S(2)}) %collective-permute-start.25) | collective-permute-done | bytes 40992 | tf_op jit(solution)/shard_map/ppermute | solution.py:526
  110.5 1.9 %collective-permute-start.26 = (f32[5,8,128]{2,1,0:T(8,128)S(1)}, f32[5,8,128]{2,1,0:T(8,128)S(1)}, u32[]{:S(2)}, u32[]{:S(2)}) collective-permute-start(f32[5,8,128]{2,1,0:T(8,128)S(1)} %get-tuple-element.89), channel_id=1, source_target_pairs={{0,16},{4,20},{8,24},{12,28},{16,0},{20,4},{24,8},{28,12},{1,17},{... | collective-permute-start | bytes 61448 | tf_op jit(solution)/shard_map/ppermute | solution.py:526
  112.4 2.4 %shard_map.131 = (f32[32,64,128]{2,1,0:T(8,128)S(1)}, f32[1,64,128]{2,1,0:T(8,128)S(1)}, f32[1,64,128]{2,1,0:T(8,128)S(1)}) custom-call(s32[128]{0:T(128)S(1)} %and_select_fusion.row_ref, f32[128,128]{1,0:T(8,128)S(1)} %get-tuple-element.74.value_ref, s32[128,128]{1,0:T(8,128)S(1)} %get-tuple-element.49.col_ref, ...), custom_call_target="tpu_custom_call", output_to_operand_aliasing={{0}: (4, {})} | custom-call | flops 536870912 | bytes 1048576 | tf_op jit(solution)/shard_map/pallas_call | solution.py:510
  114.8 0.4 collective-permute-start.21
  115.4 3.8 %collective-permute-done.27.two_ref = f32[5,8,128]{2,1,0:T(8,128)S(1)} collective-permute-done((f32[5,8,128]{2,1,0:T(8,128)S(1)}, f32[5,8,128]{2,1,0:T(8,128)S(1)}, u32[]{:S(2)}, u32[]{:S(2)}) %collective-permute-start.27) | collective-permute-done | bytes 20512 | tf_op jit(solution)/shard_map/ppermute | solution.py:526
  119.1 1.6 %collective-permute-start.28 = (f32[5,8,128]{2,1,0:T(8,128)S(1)}, f32[5,8,128]{2,1,0:T(8,128)S(1)}, u32[]{:S(2)}, u32[]{:S(2)}) collective-permute-start(f32[5,8,128]{2,1,0:T(8,128)S(1)} %shard_map.136.one_ref), channel_id=1, source_target_pairs={{0,2},{1,3},{2,0},{3,1},{4,6},{5,7},{6,4},{7,5},{8,10},{9,11},{10,... | collective-permute-start | bytes 61448 | tf_op jit(solution)/shard_map/ppermute | solution.py:526
  120.8 2.1 %collective-permute-start.22 = (f32[34,1,128]{2,1,0:T(1,128)S(1)}, f32[34,1,128]{2,1,0:T(1,128)S(1)}, u32[]{:S(2)}, u32[]{:S(2)}) collective-permute-start(f32[34,1,128]{2,1,0:T(1,128)S(1)} %get-tuple-element.78), channel_id=1, source_target_pairs={{0,1},{1,0},{2,3},{3,2},{4,5},{5,4},{6,7},{7,6},{8,9},{9,8},{10,11... | collective-permute-start | bytes 52232 | tf_op jit(solution)/shard_map/ppermute | solution.py:526
  122.9 0.7 collective-permute-start.23
  123.7 1.0 collective-permute-done.22.beside_ref
  124.6 3.8 %collective-permute-done.23.across_ref = f32[34,1,128]{2,1,0:T(1,128)S(1)} collective-permute-done((f32[34,1,128]{2,1,0:T(1,128)S(1)}, f32[34,1,128]{2,1,0:T(1,128)S(1)}, u32[]{:S(2)}, u32[]{:S(2)}) %collective-permute-start.23) | collective-permute-done | bytes 17440 | tf_op jit(solution)/shard_map/ppermute | solution.py:577
  128.5 1.3 shard_map.137
  129.8 9.5 %all_to_all.5.sum_ref = f32[32,1,128]{2,1,0:T(1,128)S(1)} all-to-all(f32[32,1,128]{2,1,0:T(1,128)S(1)} %shard_map.137), channel_id=1, replica_groups=mesh['swath'=8,'chan'=4] {'swath','chan'}, dimensions={0} | all-to-all | bytes 32768 | tf_op jit(solution)/shard_map/all_to_all | solution.py:678
  139.3 1.3 shard_map.138
  (50 shorter events, 1.2 us)
Async XLA Ops:
  1.3 26.6 %copy-start.4 = (s32[16384]{0:T(1024)S(1)}, s32[16384]{0:T(1024)}, u32[]{:S(2)}) copy-start(s32[16384]{0:T(1024)} %param.13) | copy-start | bytes 196612
  1.3 33.2 %copy-start = (bf16[16384,128]{1,0:T(8,128)(2,1)S(1)}, bf16[16384,128]{1,0:T(8,128)(2,1)}, u32[]{:S(2)}) copy-start(bf16[16384,128]{1,0:T(8,128)(2,1)} %jac_ref.5) | copy-start | bytes 12582916
  11.5 37.5 %copy-start.3 = (f32[128]{0:T(128)S(1)}, f32[128]{0:T(128)}, u32[]{:S(2)}) copy-start(f32[128]{0:T(128)} %param.16) | copy-start | bytes 1540
  11.5 1.5 %collective-permute-start.4 = (f32[2,20,8,128]{3,2,1,0:T(8,128)S(1)}, f32[2,20,8,128]{3,2,1,0:T(8,128)S(1)}, u32[]{:S(2)}, u32[]{:S(2)}) collective-permute-start(f32[2,20,8,128]{3,2,1,0:T(8,128)S(1)} %get-tuple-element.59), channel_id=1, source_target_pairs={{0,4},{4,0},{8,12},{12,8},{16,20},{20,16},{24,28},{28,24},{1,5},{5... | collective-permute-start | bytes 491528 | tf_op jit(solution)/shard_map/ppermute | solution.py:526
  13.1 7.4 %collective-permute-start.5 = (f32[2,20,8,128]{3,2,1,0:T(8,128)S(1)}, f32[2,20,8,128]{3,2,1,0:T(8,128)S(1)}, u32[]{:S(2)}, u32[]{:S(2)}) collective-permute-start(f32[2,20,8,128]{3,2,1,0:T(8,128)S(1)} %shard_map.116.one_ref), channel_id=1, source_target_pairs={{0,8},{4,12},{8,0},{12,4},{16,24},{20,28},{24,16},{28,20},{1,9},{5... | collective-permute-start | bytes 491528 | tf_op jit(solution)/shard_map/ppermute | solution.py:526
  20.5 5.7 %collective-permute-start.6 = (f32[2,20,8,128]{3,2,1,0:T(8,128)S(1)}, f32[2,20,8,128]{3,2,1,0:T(8,128)S(1)}, u32[]{:S(2)}, u32[]{:S(2)}) collective-permute-start(f32[2,20,8,128]{3,2,1,0:T(8,128)S(1)} %shard_map.117.one_ref), channel_id=1, source_target_pairs={{0,16},{4,20},{8,24},{12,28},{16,0},{20,4},{24,8},{28,12},{1,17},{... | collective-permute-start | bytes 491528 | tf_op jit(solution)/shard_map/ppermute | solution.py:526
  26.3 5.4 %collective-permute-start.7 = (f32[2,20,8,128]{3,2,1,0:T(8,128)S(1)}, f32[2,20,8,128]{3,2,1,0:T(8,128)S(1)}, u32[]{:S(2)}, u32[]{:S(2)}) collective-permute-start(f32[2,20,8,128]{3,2,1,0:T(8,128)S(1)} %shard_map.118.one_ref), channel_id=1, source_target_pairs={{0,1},{1,0},{2,3},{3,2},{4,5},{5,4},{6,7},{7,6},{8,9},{9,8},{10,11... | collective-permute-start | bytes 491528 | tf_op jit(solution)/shard_map/ppermute | solution.py:526
  31.7 11.8 %collective-permute-start.8 = (f32[2,20,8,128]{3,2,1,0:T(8,128)S(1)}, f32[2,20,8,128]{3,2,1,0:T(8,128)S(1)}, u32[]{:S(2)}, u32[]{:S(2)}) collective-permute-start(f32[2,20,8,128]{3,2,1,0:T(8,128)S(1)} %shard_map.119.one_ref), channel_id=1, source_target_pairs={{0,2},{1,3},{2,0},{3,1},{4,6},{5,7},{6,4},{7,5},{8,10},{9,11},{10,... | collective-permute-start | bytes 491528 | tf_op jit(solution)/shard_map/ppermute | solution.py:526
  37.0 2.5 %collective-permute-start = (f32[2,64,128]{2,1,0:T(8,128)S(1)}, f32[2,64,128]{2,1,0:T(8,128)S(1)}, u32[]{:S(2)}, u32[]{:S(2)}) collective-permute-start(f32[2,64,128]{2,1,0:T(8,128)S(1)} %get-tuple-element.51), channel_id=1, source_target_pairs={{0,4},{4,0},{8,12},{12,8},{16,20},{20,16},{24,28},{28,24},{1,5},{5... | collective-permute-start | bytes 196616 | tf_op jit(solution)/shard_map/ppermute | solution.py:526
  37.0 4.7 %collective-permute-start.1 = (f32[2,64,128]{2,1,0:T(8,128)S(1)}, f32[2,64,128]{2,1,0:T(8,128)S(1)}, u32[]{:S(2)}, u32[]{:S(2)}) collective-permute-start(f32[2,64,128]{2,1,0:T(8,128)S(1)} %get-tuple-element.52), channel_id=1, source_target_pairs={{4,8},{12,16},{20,24},{28,0},{8,4},{16,12},{24,20},{0,28},{5,9},{1... | collective-permute-start | bytes 196616 | tf_op jit(solution)/shard_map/ppermute | solution.py:572
  41.8 4.0 %collective-permute-start.2 = (f32[36,2,128]{2,1,0:T(2,128)S(1)}, f32[36,2,128]{2,1,0:T(2,128)S(1)}, u32[]{:S(2)}, u32[]{:S(2)}) collective-permute-start(f32[36,2,128]{2,1,0:T(2,128)S(1)} %get-tuple-element.53), channel_id=1, source_target_pairs={{0,1},{1,0},{2,3},{3,2},{4,5},{5,4},{6,7},{7,6},{8,9},{9,8},{10,11... | collective-permute-start | bytes 110600 | tf_op jit(solution)/shard_map/ppermute | solution.py:526
  43.2 5.8 %collective-permute-start.3 = (f32[36,2,128]{2,1,0:T(2,128)S(1)}, f32[36,2,128]{2,1,0:T(2,128)S(1)}, u32[]{:S(2)}, u32[]{:S(2)}) collective-permute-start(f32[36,2,128]{2,1,0:T(2,128)S(1)} %get-tuple-element.54), channel_id=1, source_target_pairs={{1,2},{3,0},{2,1},{0,3},{5,6},{7,4},{6,5},{4,7},{9,10},{11,8},{10,... | collective-permute-start | bytes 110600 | tf_op jit(solution)/shard_map/ppermute | solution.py:577
  43.5 12.7 %collective-permute-start.9 = (f32[20,8,128]{2,1,0:T(8,128)S(1)}, f32[20,8,128]{2,1,0:T(8,128)S(1)}, u32[]{:S(2)}, u32[]{:S(2)}) collective-permute-start(f32[20,8,128]{2,1,0:T(8,128)S(1)} %get-tuple-element.60.mine_ref.zb_ref.zm_ref), channel_id=1, source_target_pairs={{0,4},{4,0},{8,12},{12,8},{16,20},{20,16},{24,28},{28,24},{1,5},{5... | collective-permute-start | bytes 245768 | tf_op jit(solution)/shard_map/ppermute | solution.py:526
  56.2 21.3 %copy-start.1 = (bf16[16384,128]{1,0:T(8,128)(2,1)S(1)}, bf16[16384,128]{1,0:T(8,128)(2,1)}, u32[]{:S(2)}) copy-start(bf16[16384,128]{1,0:T(8,128)(2,1)} %jac_ref.5) | copy-start | bytes 12582916
  62.4 1.3 collective-permute-start.14
  63.8 4.6 %collective-permute-start.15 = (f32[20,8,128]{2,1,0:T(8,128)S(1)}, f32[20,8,128]{2,1,0:T(8,128)S(1)}, u32[]{:S(2)}, u32[]{:S(2)}) collective-permute-start(f32[20,8,128]{2,1,0:T(8,128)S(1)} %shard_map.125.one_ref), channel_id=1, source_target_pairs={{0,8},{4,12},{8,0},{12,4},{16,24},{20,28},{24,16},{28,20},{1,9},{5... | collective-permute-start | bytes 245768 | tf_op jit(solution)/shard_map/ppermute | solution.py:526
  68.4 4.5 %collective-permute-start.16 = (f32[20,8,128]{2,1,0:T(8,128)S(1)}, f32[20,8,128]{2,1,0:T(8,128)S(1)}, u32[]{:S(2)}, u32[]{:S(2)}) collective-permute-start(f32[20,8,128]{2,1,0:T(8,128)S(1)} %shard_map.126.one_ref), channel_id=1, source_target_pairs={{0,16},{4,20},{8,24},{12,28},{16,0},{20,4},{24,8},{28,12},{1,17},{... | collective-permute-start | bytes 245768 | tf_op jit(solution)/shard_map/ppermute | solution.py:526
  72.9 4.5 %collective-permute-start.17 = (f32[20,8,128]{2,1,0:T(8,128)S(1)}, f32[20,8,128]{2,1,0:T(8,128)S(1)}, u32[]{:S(2)}, u32[]{:S(2)}) collective-permute-start(f32[20,8,128]{2,1,0:T(8,128)S(1)} %shard_map.127.one_ref), channel_id=1, source_target_pairs={{0,1},{1,0},{2,3},{3,2},{4,5},{5,4},{6,7},{7,6},{8,9},{9,8},{10,11... | collective-permute-start | bytes 245768 | tf_op jit(solution)/shard_map/ppermute | solution.py:526
  77.4 11.8 %collective-permute-start.18 = (f32[20,8,128]{2,1,0:T(8,128)S(1)}, f32[20,8,128]{2,1,0:T(8,128)S(1)}, u32[]{:S(2)}, u32[]{:S(2)}) collective-permute-start(f32[20,8,128]{2,1,0:T(8,128)S(1)} %shard_map.128.one_ref), channel_id=1, source_target_pairs={{0,2},{1,3},{2,0},{3,1},{4,6},{5,7},{6,4},{7,5},{8,10},{9,11},{10,... | collective-permute-start | bytes 245768 | tf_op jit(solution)/shard_map/ppermute | solution.py:526
  79.9 2.1 %collective-permute-start.10 = (f32[2,64,128]{2,1,0:T(8,128)S(1)}, f32[2,64,128]{2,1,0:T(8,128)S(1)}, u32[]{:S(2)}, u32[]{:S(2)}) collective-permute-start(f32[2,64,128]{2,1,0:T(8,128)S(1)} %get-tuple-element.65), channel_id=1, source_target_pairs={{0,4},{4,0},{8,12},{12,8},{16,20},{20,16},{24,28},{28,24},{1,5},{5... | collective-permute-start | bytes 196616 | tf_op jit(solution)/shard_map/ppermute | solution.py:526
  80.0 4.7 %collective-permute-start.11 = (f32[2,64,128]{2,1,0:T(8,128)S(1)}, f32[2,64,128]{2,1,0:T(8,128)S(1)}, u32[]{:S(2)}, u32[]{:S(2)}) collective-permute-start(f32[2,64,128]{2,1,0:T(8,128)S(1)} %get-tuple-element.66), channel_id=1, source_target_pairs={{4,8},{12,16},{20,24},{28,0},{8,4},{16,12},{24,20},{0,28},{5,9},{1... | collective-permute-start | bytes 196616 | tf_op jit(solution)/shard_map/ppermute | solution.py:572
  84.7 4.6 %collective-permute-start.12 = (f32[36,2,128]{2,1,0:T(2,128)S(1)}, f32[36,2,128]{2,1,0:T(2,128)S(1)}, u32[]{:S(2)}, u32[]{:S(2)}) collective-permute-start(f32[36,2,128]{2,1,0:T(2,128)S(1)} %get-tuple-element.67), channel_id=1, source_target_pairs={{0,1},{1,0},{2,3},{3,2},{4,5},{5,4},{6,7},{7,6},{8,9},{9,8},{10,11... | collective-permute-start | bytes 110600 | tf_op jit(solution)/shard_map/ppermute | solution.py:526
  85.7 5.8 %collective-permute-start.13 = (f32[36,2,128]{2,1,0:T(2,128)S(1)}, f32[36,2,128]{2,1,0:T(2,128)S(1)}, u32[]{:S(2)}, u32[]{:S(2)}) collective-permute-start(f32[36,2,128]{2,1,0:T(2,128)S(1)} %get-tuple-element.68), channel_id=1, source_target_pairs={{1,2},{3,0},{2,1},{0,3},{5,6},{7,4},{6,5},{4,7},{9,10},{11,8},{10,... | collective-permute-start | bytes 110600 | tf_op jit(solution)/shard_map/ppermute | solution.py:577
  89.2 9.6 %collective-permute-start.19 = (f32[20,8,128]{2,1,0:T(8,128)S(1)}, f32[20,8,128]{2,1,0:T(8,128)S(1)}, u32[]{:S(2)}, u32[]{:S(2)}) collective-permute-start(f32[20,8,128]{2,1,0:T(8,128)S(1)} %get-tuple-element.73.mine_ref.ub_ref.um_ref), channel_id=1, source_target_pairs={{0,4},{4,0},{8,12},{12,8},{16,20},{20,16},{24,28},{28,24},{1,5},{5... | collective-permute-start | bytes 245768 | tf_op jit(solution)/shard_map/ppermute | solution.py:526
  98.8 13.5 %copy-start.2 = (bf16[16384,128]{1,0:T(8,128)(2,1)S(1)}, bf16[16384,128]{1,0:T(8,128)(2,1)}, u32[]{:S(2)}) copy-start(bf16[16384,128]{1,0:T(8,128)(2,1)} %jac_ref.5) | copy-start | bytes 12582916
  105.1 1.3 collective-permute-start.24
  106.4 4.1 %collective-permute-start.25 = (f32[10,8,128]{2,1,0:T(8,128)S(1)}, f32[10,8,128]{2,1,0:T(8,128)S(1)}, u32[]{:S(2)}, u32[]{:S(2)}) collective-permute-start(f32[10,8,128]{2,1,0:T(8,128)S(1)} %get-tuple-element.87), channel_id=1, source_target_pairs={{0,8},{4,12},{8,0},{12,4},{16,24},{20,28},{24,16},{28,20},{1,9},{5... | collective-permute-start | bytes 122888 | tf_op jit(solution)/shard_map/ppermute | solution.py:526
  110.5 4.8 %collective-permute-start.26 = (f32[5,8,128]{2,1,0:T(8,128)S(1)}, f32[5,8,128]{2,1,0:T(8,128)S(1)}, u32[]{:S(2)}, u32[]{:S(2)}) collective-permute-start(f32[5,8,128]{2,1,0:T(8,128)S(1)} %get-tuple-element.89), channel_id=1, source_target_pairs={{0,16},{4,20},{8,24},{12,28},{16,0},{20,4},{24,8},{28,12},{1,17},{... | collective-permute-start | bytes 61448 | tf_op jit(solution)/shard_map/ppermute | solution.py:526
  114.8 6.0 %collective-permute-start.20 = (f32[1,64,128]{2,1,0:T(8,128)S(1)}, f32[1,64,128]{2,1,0:T(8,128)S(1)}, u32[]{:S(2)}, u32[]{:S(2)}) collective-permute-start(f32[1,64,128]{2,1,0:T(8,128)S(1)} %get-tuple-element.76), channel_id=1, source_target_pairs={{0,4},{4,0},{8,12},{12,8},{16,20},{20,16},{24,28},{28,24},{1,5},{5... | collective-permute-start | bytes 98312 | tf_op jit(solution)/shard_map/ppermute | solution.py:526
  114.8 5.9 %collective-permute-start.21 = (f32[1,64,128]{2,1,0:T(8,128)S(1)}, f32[1,64,128]{2,1,0:T(8,128)S(1)}, u32[]{:S(2)}, u32[]{:S(2)}) collective-permute-start(f32[1,64,128]{2,1,0:T(8,128)S(1)} %get-tuple-element.77), channel_id=1, source_target_pairs={{4,8},{12,16},{20,24},{28,0},{8,4},{16,12},{24,20},{0,28},{5,9},{1... | collective-permute-start | bytes 98312 | tf_op jit(solution)/shard_map/ppermute | solution.py:572
  115.3 3.8 %collective-permute-start.27 = (f32[5,8,128]{2,1,0:T(8,128)S(1)}, f32[5,8,128]{2,1,0:T(8,128)S(1)}, u32[]{:S(2)}, u32[]{:S(2)}) collective-permute-start(f32[5,8,128]{2,1,0:T(8,128)S(1)} %shard_map.135.one_ref), channel_id=1, source_target_pairs={{0,1},{1,0},{2,3},{3,2},{4,5},{5,4},{6,7},{7,6},{8,9},{9,8},{10,11... | collective-permute-start | bytes 61448 | tf_op jit(solution)/shard_map/ppermute | solution.py:526
  119.1 9.3 %collective-permute-start.28 = (f32[5,8,128]{2,1,0:T(8,128)S(1)}, f32[5,8,128]{2,1,0:T(8,128)S(1)}, u32[]{:S(2)}, u32[]{:S(2)}) collective-permute-start(f32[5,8,128]{2,1,0:T(8,128)S(1)} %shard_map.136.one_ref), channel_id=1, source_target_pairs={{0,2},{1,3},{2,0},{3,1},{4,6},{5,7},{6,4},{7,5},{8,10},{9,11},{10,... | collective-permute-start | bytes 61448 | tf_op jit(solution)/shard_map/ppermute | solution.py:526
  120.8 3.8 %collective-permute-start.22 = (f32[34,1,128]{2,1,0:T(1,128)S(1)}, f32[34,1,128]{2,1,0:T(1,128)S(1)}, u32[]{:S(2)}, u32[]{:S(2)}) collective-permute-start(f32[34,1,128]{2,1,0:T(1,128)S(1)} %get-tuple-element.78), channel_id=1, source_target_pairs={{0,1},{1,0},{2,3},{3,2},{4,5},{5,4},{6,7},{7,6},{8,9},{9,8},{10,11... | collective-permute-start | bytes 52232 | tf_op jit(solution)/shard_map/ppermute | solution.py:526
  122.9 5.5 %collective-permute-start.23 = (f32[34,1,128]{2,1,0:T(1,128)S(1)}, f32[34,1,128]{2,1,0:T(1,128)S(1)}, u32[]{:S(2)}, u32[]{:S(2)}) collective-permute-start(f32[34,1,128]{2,1,0:T(1,128)S(1)} %get-tuple-element.79), channel_id=1, source_target_pairs={{1,2},{3,0},{2,1},{0,3},{5,6},{7,4},{6,5},{4,7},{9,10},{11,8},{10,... | collective-permute-start | bytes 52232 | tf_op jit(solution)/shard_map/ppermute | solution.py:577
